TPU v7x, 128 devices: a whole 4x4x4 slice. The times are simulated.
128 devices in a mesh: ctx: 8 (over z, y_lo), grp: 4 (over y_hi, core), tp: 4 (over x).
Axes of the slice: x: 4, y: 4 (y_hi: 2, y_lo: 2; y = y_hi * 2 + y_lo), z: 4, core: 2. Of those that a mesh axis runs over, the one named last changes fastest.
Arguments:
- tokens: bfloat16 [16384, 4608], P(('grp', 'ctx')), parts along dimension 0, may hold values from -6 to 6
- token_pos: int32 [16384], P(('grp', 'ctx')), parts along dimension 0, may hold values from 0 to 4095, as said below
- norm_gain: float32 [4608], replicated, may hold values from 0.1 to 1.9
- query_weight: bfloat16 [4608, 4096], P('ctx', 'tp'), may hold values from -0.09375 to 0.09375
- key_weight: bfloat16 [4608, 2048], P('ctx', 'tp'), may hold values from -0.09375 to 0.09375
- value_weight: bfloat16 [4608, 2048], P('ctx', 'tp'), may hold values from -0.09375 to 0.09375
Outputs:
- attended: bfloat16 [16384, 4096], P(('grp', 'ctx'), 'tp'), parts along dimension 0
There are 4 independent parts, one for each index of `grp`. A program takes and returns all parts, laid end to end along the dimension named above; an argument that names none is the same for every part. Nothing has to cross between parts.
Inputs may be any that keep to these rules, and one draw needn't show every extreme that they name: `token_pos`: the 512 rows of each index of ctx form two runs of 256 consecutive ascending positions, each starting at a multiple of 256; every position of the sequence occurs exactly once.
All inputs are finite; a program needn't handle non-finite values.
Results may differ from a plain program's by a relative error of at most 0.0077.
Values may be sent and summed in bfloat16 or wider, within the bound.
A program may use at most 128 MiB of HBM per device.

v0:
```python
import math

import jax
import jax.numpy as jnp
from jax import lax
from jax.sharding import PartitionSpec as P

HEAD_DIM = 128


query_scale = 144.0 ** (-0.5)


def side_by_side(arrays, axis, dim, along):
    ends, at = ([], 0)
    for a in arrays[:-1]:
        at += a.shape[along]
        ends.append(at)
    both = jnp.concatenate(arrays, axis=along)
    return tuple(jnp.split(lax.all_gather(both, axis, axis=dim, tiled=True), ends, axis=along))


def rotate(field, positions):
    half = field.shape[-1] // 2
    freq = 10000.0 ** (-jnp.arange(half, dtype=jnp.float32) * 2.0 / field.shape[-1])
    angle = positions.astype(jnp.float32)[:, None] * freq[None, :]
    cosine = jnp.cos(angle)[:, None, :]
    sine = jnp.sin(angle)[:, None, :]
    first = field[..., :half]
    second = field[..., half:]
    return jnp.concatenate([first * cosine - second * sine, second * cosine + first * sine], -1)


def make_compute(query_run, pos_run, key_part, value_part, pos_part):

    def compute(state):
        numerator, total = state
        scores = jnp.einsum(
            "ngrd,mgd->grnm", query_run, key_part, preferred_element_type=jnp.float32
        )
        capped = 50.0 * jnp.tanh(scores / 50.0)
        allowed = pos_part[None, None, None, :] <= pos_run[None, None, :, None]
        weights = jnp.where(allowed, jnp.exp(capped), 0.0).astype(jnp.bfloat16)
        numerator = numerator + jnp.einsum(
            "grnm,mgd->ngrd", weights, value_part, preferred_element_type=jnp.float32
        )
        total = total + jnp.sum(weights.astype(jnp.float32), -1)
        return (numerator, total)

    return compute


def on_device(tokens, token_pos, norm_gain, query_weight, key_weight, value_weight):
    rows = tokens.shape[0]
    run_rows = rows // 2
    inputs = tokens.astype(jnp.float32)
    normed = (
        inputs
        * lax.rsqrt(jnp.mean(inputs * inputs, -1, keepdims=True) + 1e-06)
        * norm_gain[None, :]
    ).astype(jnp.bfloat16)

    def add_rows(piece):
        return jnp.dot(normed, piece, preferred_element_type=jnp.float32)

    pieces = side_by_side((query_weight, key_weight, value_weight), "ctx", 0, 1)
    query_sum = add_rows(pieces[0])
    key_sum = add_rows(pieces[1])
    value_sum = add_rows(pieces[2])
    groups = key_weight.shape[1] // HEAD_DIM
    queries = rotate(query_sum.reshape(rows, 2 * groups, HEAD_DIM), token_pos) * query_scale
    queries = queries.astype(jnp.bfloat16).reshape(rows, groups, 2, HEAD_DIM)
    keys = (
        rotate(key_sum.reshape(rows, groups, HEAD_DIM), token_pos)
        .astype(jnp.bfloat16)
        .reshape(rows, groups * HEAD_DIM)
    )
    values = value_sum.astype(jnp.bfloat16)
    query_runs = [
        queries[run_index * run_rows : (run_index + 1) * run_rows] for run_index in range(2)
    ]
    pos_runs = [
        token_pos[run_index * run_rows : (run_index + 1) * run_rows] for run_index in range(2)
    ]
    run_initial = (
        jnp.zeros((run_rows, groups, 2, HEAD_DIM), jnp.float32),
        jnp.zeros((groups, 2, run_rows), jnp.float32),
    )
    initial = (run_initial, run_initial)
    key_rows, value_rows, key_pos = (
        *side_by_side((keys, values), "ctx", 0, 1),
        lax.all_gather(token_pos, "ctx", axis=0, tiled=True),
    )
    length = key_rows.shape[0]
    width = math.gcd(length, run_rows)

    def one_block(index, acc):
        key_part = lax.dynamic_slice_in_dim(key_rows, index * width, width, 0).reshape(
            width, groups, HEAD_DIM
        )
        value_part = lax.dynamic_slice_in_dim(value_rows, index * width, width, 0).reshape(
            width, groups, HEAD_DIM
        )
        pos_part = lax.dynamic_slice_in_dim(key_pos, index * width, width, 0)
        updated = []
        for run_index in range(2):
            compute = make_compute(
                query_runs[run_index], pos_runs[run_index], key_part, value_part, pos_part
            )
            state = compute(acc[run_index])
            updated.append(state)
        return (updated[0], updated[1])

    finished = lax.fori_loop(0, length // width, one_block, initial)
    numerator = jnp.concatenate([finished[0][0], finished[1][0]], 0)
    total = jnp.concatenate([finished[0][1], finished[1][1]], 2)
    attended = numerator / jnp.transpose(total, (2, 0, 1))[..., None]
    return attended.astype(jnp.bfloat16).reshape(rows, 2 * groups * HEAD_DIM)


def solution(mesh):
    in_specs = (
        P(("grp", "ctx"), None),
        P(("grp", "ctx")),
        P(),
        P("ctx", "tp"),
        P("ctx", "tp"),
        P("ctx", "tp"),
    )
    out_specs = P(("grp", "ctx"), "tp")
    return jax.shard_map(
        on_device, mesh=mesh, in_specs=in_specs, out_specs=out_specs, check_vma=False
    )
```

profile of v0, /device:TPU:1, one launch (start us, length us, event | category | flops | bytes accessed | tf_op | source)
XLA Modules:
  0.0 664.0 jit_solution(15635484871091803237)
XLA Ops:
  6.5 3.3 pad_maximum_fusion
  10.5 3.3 fusion.4
  14.4 363.5 %all-gather.4.cloned.1.call-done = bf16[4608,2048]{1,0:T(8,128)(2,1)} async-done(((bf16[576,2048]{1,0:T(8,128)(2,1)}), bf16[4608,2048]{1,0:T(8,128)(2,1)}) %all-gather.4.cloned.1.call-update) | async-done | bytes 18874384 | tf_op jit(solution)/shard_map/all_gather | solution.py:20
  378.0 6.5 fusion.11
  384.7 6.5 fusion.18
  391.2 1.0 pad_maximum_fusion.1
  392.6 21.1 %all-gather = s32[8,1,512]{2,1,0:T(1,128)S(1)} all-gather(s32[1,1,512]{2,1,0:T(1,128)S(1)} %bitcast.84), channel_id=1, replica_groups=mesh['ctx'=8,'grp'=4,'tp'=4] {'ctx'}, dimensions={0}, use_global_device_ids=true | all-gather | bytes 18432 | tf_op jit(solution)/shard_map/all_gather | solution.py:92
  413.7 9.2 %fusion.15 = f32[64,8,8,128]{3,1,2,0:T(8,128)S(1)} fusion(bf16[4608,2048]{1,0:T(8,128)(2,1)} %all-gather.4.cloned.1.call-done, bf16[512,4608]{1,0:T(8,128)(2,1)} %param.8, f32[4608]{0:T(1024)S(1)} %copy-done.1, f32[512]{0:T(512)S(1)} %add_rsqrt_fusion), kind=kOutput, calls=%fused_computation.34 | convolution fusion | flops 4841275392 | bytes 16273408 | tf_op jit(solution)/shard_map/dot_general | solution.py:64
  423.4 1.1 multiply_subtract_fusion
  425.3 136.7 %all-gather.6.cloned.1.call-done = bf16[4096,1024]{0,1:T(8,128)(2,1)} async-done(((bf16[512,1024]{0,1:T(8,128)(2,1)}), bf16[4096,1024]{0,1:T(8,128)(2,1)}) %all-gather.6.cloned.1.call-update) | async-done | bytes 8388624 | tf_op jit(solution)/shard_map/all_gather | solution.py:20
  562.0 5.9 fusion.24
  567.9 76.4 %while.20 = (s32[]{:T(128)}, f32[256,4,2,128]{0,3,2,1:T(8,128)S(1)}, f32[4,2,256]{2,1,0:T(2,128)S(1)}, f32[256,4,2,128]{0,3,2,1:T(8,128)S(1)}, f32[4,2,256]{2,1,...) while((s32[]{:T(128)}, ...), condition=%wide.region_4.5_spmd.clone, body=%wide.region_1.4_spmd.clone.sunk | while | flops 544346112 | bytes 11867363 | solution.py:114
  568.1 1.0 constant_dynamic-slice_fusion.5
  569.1 1.0 constant_dynamic-slice_fusion.4
  587.2 1.0 constant_dynamic-slice_fusion.5
  588.2 1.0 constant_dynamic-slice_fusion.4
  615.9 1.0 constant_dynamic-slice_fusion.5
  620.7 1.0 constant_dynamic-slice_fusion.5
  630.2 1.0 constant_dynamic-slice_fusion.5
  644.3 1.3 copy.44
  646.1 4.0 div.37
  650.0 2.9 div.38
  653.0 1.3 copy.45
  654.3 2.9 fusion.14
  (165 shorter events, 72.1 us)
Async XLA Ops:
  6.5 371.4 %all-gather.4.cloned.1.call-start = ((), (), s32[]{:S(2)}) async-start(), calls=%async_computation | async-start | bytes 21233664 | tf_op jit(solution)/shard_map/all_gather | solution.py:20
  9.8 0.7 copy-start
  9.8 552.1 %all-gather.6.cloned.1.call-start = ((), (), s32[]{:S(2)}) async-start(), calls=%async_computation.1 | async-start | bytes 9437184 | tf_op jit(solution)/shard_map/all_gather | solution.py:20
  10.5 367.4 %copy-start.1 = (f32[4608]{0:T(1024)S(1)}, f32[4608]{0:T(1024)}, u32[]{:S(2)}) copy-start(f32[4608]{0:T(1024)} %param.10) | copy-start | bytes 55300
Sparse Core Ops, SparseCore 0:
  10.0 367.9 all-gather.3
  392.4 169.4 all-gather.5
where the time goes:
time: 665 us; the launch traced here: 664 us
  waiting for transfers between devices  500 us (75%)
  matrix products  62.5 us (9%)
  local copies, waits for them, and re-layouts  49.9 us (8%)
  blocking collectives  21.1 us (3%)
  other arithmetic  15.7 us (2%)
  between operations  13.6 us (2%)
    all_gather x2, waiting for transfers between devices, side_by_side(): lax.all_gather(both, axis, axis=dim, tiled=True)  500 us
    dot_general x32, matrix products, compute(): jnp.einsum('ngrd,mgd->grnm', query_run, key_part, preferred_element_type=...  28 us
    dot_general x3, matrix products, add_rows(): return jnp.dot(normed, piece, preferred_element_type=jnp.float32)  22.2 us
    all_gather x1, blocking collectives, on_device(): lax.all_gather(token_pos, 'ctx', axis=0, tiled=True)  21.1 us
    dynamic_slice x16, local copies, waits for them, and re-layouts, one_block(): lax.dynamic_slice_in_dim(key_rows, index * width, width, 0)  15.6 us
    dynamic_slice x16, local copies, waits for them, and re-layouts, one_block(): lax.dynamic_slice_in_dim(value_rows, index * width, width, 0)  15.6 us
  transfers between devices with their start and end apart: 2, of which 2 were waited for; matrix products, arithmetic and copies ran while one was open for 2% of the time, Pallas kernels for 0%

commit v1 on v0

v1 whole, which is shorter than its diff:
```python
import functools
import math

import jax
import jax.numpy as jnp
from jax import lax
from jax.experimental import pallas as pl
from jax.experimental.pallas import tpu as pltpu
from jax.sharding import PartitionSpec as P

HEAD_DIM = 128
MESH = pl.DeviceIdType.MESH
query_scale = 144.0 ** (-0.5)
EXP_SCALE = 50.0 * math.log2(math.e)
SHARDS = 8
SPLIT_KV = 144
SPLIT_Q = 112


def tile(index, size):
    return pl.ds(pl.multiple_of(index * size, size), size)


def kernel(
    x_hbm, gain_ref, wq_hbm, wk_hbm, wv_hbm, cos_ref, sin_ref, pos_ref,
    o_ref,
    xv, normed, wkv, wq, acc, posb, qpos, kvb, kvx, qb, qx, num, osend, orecv,
    local_sem, send_sem, wkv_sem, wq_sem, kv_sem, q_sem, o_sem, pos_sem,
):
    ctx = lax.axis_index("ctx")
    grp = lax.axis_index("grp")
    z, par = ctx // 2, ctx % 2
    y_hi, core = grp // 2, grp % 2
    up, down, far = (z + 1) % 4, (z + 3) % 4, (z + 2) % 4
    other = 1 - par
    pair = z * 2 + other
    to_up = {"ctx": up * 2 + par}
    to_down = {"ctx": down * 2 + par}
    to_pair = {"ctx": pair}
    to_cross = {"ctx": pair, "grp": (1 - y_hi) * 2 + core}
    to_peer = {"grp": y_hi * 2 + (1 - core)}
    group = [{"ctx": (ctx + i) % SHARDS} for i in range(1, SHARDS)]

    rows, feats = xv.shape
    depth = wq.shape[1]
    nq, nk = wq_hbm.shape[1], wk_hbm.shape[1]
    hd = HEAD_DIM
    half_rows = rows // 2

    barrier = pltpu.get_barrier_semaphore()
    for dev in group + [to_cross, to_peer]:
        pl.semaphore_signal(barrier, inc=1, device_id=dev, device_id_type=MESH)
    loads = [
        pltpu.make_async_copy(wk_hbm, wkv.at[ctx, :, pl.ds(0, nk)], local_sem.at[0]),
        pltpu.make_async_copy(wv_hbm, wkv.at[ctx, :, pl.ds(nk, nk)], local_sem.at[1]),
        pltpu.make_async_copy(x_hbm, xv, local_sem.at[2]),
        pltpu.make_async_copy(wq_hbm, wq.at[ctx], local_sem.at[3]),
    ]
    for load in loads:
        load.start()
    loads[0].wait()
    loads[1].wait()
    pl.semaphore_wait(barrier, SHARDS + 1)

    sends = []

    def copy_of(src, dst, recv, dev, at):
        return pltpu.make_async_remote_copy(
            src_ref=src, dst_ref=dst, send_sem=send_sem.at[at], recv_sem=recv,
            device_id=dev, device_id_type=MESH,
        )

    def send(src, dst, recv, dev):
        copy = copy_of(src, dst, recv, dev, len(sends))
        copy.start()
        sends.append(copy)

    def await_copy(dst, recv):
        copy_of(dst, dst, recv, to_peer, 0).wait_recv()

    class Gather:
        def __init__(self, buf, sem, split):
            self.buf, self.sem, self.split = buf, sem, split

        def piece(self, shard, owner, kind):
            base = owner * (depth // 2) + (self.split if kind else 0)
            size = depth // 2 - self.split if kind else self.split
            return self.buf.at[shard, pl.ds(pl.multiple_of(base, 16), size), :]

        def send(self, shard, kind, *devs):
            ref = self.piece(shard, core, kind)
            for dev in devs:
                send(ref, ref, self.sem.at[shard, core * 2 + kind], dev)

        def wait(self, shard, kind, owner=core):
            await_copy(self.piece(shard, owner, kind), self.sem.at[shard, owner * 2 + kind])

        def relay(self, shard, kind, *devs):
            self.wait(shard, kind)
            self.send(shard, kind, *devs)

        def complete(self, *shards):
            for s in shards:
                self.wait(s, 0, 1 - core)
                self.wait(s, 1, 1 - core)

    A, B = 0, 1
    own = ctx
    up_own, up_oth = up * 2 + par, up * 2 + other
    down_own, down_oth = down * 2 + par, down * 2 + other
    far_own, far_oth = far * 2 + par, far * 2 + other

    gkv = Gather(wkv, wkv_sem, SPLIT_KV)
    gq = Gather(wq, wq_sem, SPLIT_Q)

    def add(buf, shard, at, first=False):
        width = 256

        @pl.loop(0, buf.shape[2] // width)
        def _(j):
            cols = tile(j, width)
            part = jnp.dot(normed[shard], buf[shard, :, cols], preferred_element_type=jnp.float32)
            acc[at, :, cols] = part if first else acc[at, :, cols] + part

    def add_kv(*shards, first=False):
        for s in shards:
            add(wkv, s, 0, first)

    def add_q(*shards, first=False):
        for s in shards:
            add(wq, s, 1, first)

    gkv.send(own, A, to_up, to_pair)
    gkv.send(own, B, to_down, to_cross)
    gkv.send(own, B, to_up)
    gkv.send(own, A, to_down)
    for dev in group:
        send(pos_ref, posb.at[ctx], pos_sem.at[ctx], dev)
    posb[ctx] = pos_ref[...]

    loads[2].wait()
    block = 64

    @pl.loop(0, rows // block)
    def _(i):
        at = tile(i, block)
        value = xv[at, :].astype(jnp.float32)
        scale = lax.rsqrt(jnp.mean(value * value, -1, keepdims=True) + 1e-06)
        out = (value * scale * gain_ref[...]).astype(jnp.bfloat16)
        for s in range(SHARDS):
            normed[s, at, :] = out[:, s * depth : (s + 1) * depth]

    loads[3].wait()
    add_kv(own, first=True)

    gkv.relay(down_own, A, to_up, to_pair, to_peer)
    gkv.relay(up_own, B, to_down, to_cross, to_peer)
    gkv.relay(pair, A, to_peer)
    gkv.relay(pair, B, to_peer)
    gkv.complete(pair)
    add_kv(pair)

    gkv.relay(down_own, B, to_cross, to_peer)
    gkv.relay(up_own, A, to_pair, to_peer)
    gq.send(own, A, to_up)
    gq.send(own, B, to_down)
    gq.send(own, B, to_up)
    gq.send(own, A, to_down)
    gkv.relay(down_oth, A, to_peer)
    gkv.relay(up_oth, B, to_peer)
    gkv.complete(down_own, up_own)
    add_kv(down_own, up_own)

    gkv.relay(far_own, A, to_pair, to_peer)
    gkv.relay(far_own, B, to_cross, to_peer)
    gq.send(own, A, to_pair)
    gq.send(own, B, to_cross)
    gkv.relay(up_oth, A, to_peer)
    gkv.relay(down_oth, B, to_peer)
    gkv.complete(down_oth, up_oth, far_own)
    add_kv(down_oth, up_oth, far_own)
    add_q(own, first=True)

    gkv.relay(far_oth, A, to_peer)
    gkv.relay(far_oth, B, to_peer)
    gq.relay(down_own, A, to_up, to_peer)
    gq.relay(up_own, B, to_down, to_cross, to_peer)
    gkv.complete(far_oth)
    add_kv(far_oth)

    def rope(u):
        return u * cos_ref[...] + pltpu.roll(u, hd // 2, 1) * sin_ref[...]

    for h in range(2):
        for ref, base in ((kvb.at[ctx], par * 2), (kvx, other * 2)):
            ref[:, h * hd : (h + 1) * hd] = rope(acc[0, :, tile(base + h, hd)]).astype(jnp.bfloat16)
            ref[:, (2 + h) * hd : (3 + h) * hd] = acc[0, :, tile(nk // hd + base + h, hd)].astype(
                jnp.bfloat16
            )

    def kv_half(ref, half):
        return ref.at[pl.ds(half * half_rows, half_rows), :]

    def kv_send(src, blk, half, dev):
        send(kv_half(src, half), kv_half(kvb.at[blk], half), kv_sem.at[blk, half], dev)

    def kv_wait(blk, half):
        await_copy(kv_half(kvb.at[blk], half), kv_sem.at[blk, half])

    for half in range(2):
        kv_send(kvx, ctx, half, to_pair)
    for half in range(2):
        kv_send(kvb.at[ctx], ctx, half, to_up)
        kv_send(kvb.at[ctx], ctx, 1 - half, to_down)
    gq.send(down_own, A, to_pair)

    gq.relay(down_own, B, to_cross, to_peer)
    gq.relay(up_own, A, to_pair, to_peer)
    gq.relay(pair, A, to_peer)
    gq.relay(pair, B, to_peer)
    gq.complete(down_own, up_own)
    add_q(down_own, up_own)
    gq.relay(far_own, A, to_pair, to_peer)
    gq.relay(far_own, B, to_cross, to_peer)
    gq.complete(pair)
    add_q(pair)
    kv_wait(pair, 0)
    kv_send(kvb.at[pair], pair, 0, to_up)
    kv_wait(pair, 1)
    kv_send(kvb.at[pair], pair, 1, to_down)
    kv_send(kvb.at[pair], pair, 1, to_up)
    kv_send(kvb.at[pair], pair, 0, to_down)
    gq.relay(down_oth, A, to_peer)
    gq.relay(up_oth, B, to_peer)
    gq.complete(far_own)
    add_q(far_own)
    kv_wait(down_own, 0)
    kv_send(kvb.at[down_own], down_own, 0, to_up)
    kv_wait(up_own, 1)
    kv_send(kvb.at[up_own], up_own, 1, to_down)
    kv_wait(down_own, 1)
    kv_wait(up_own, 0)
    gq.relay(up_oth, A, to_peer)
    gq.relay(down_oth, B, to_peer)
    gq.complete(down_oth, up_oth)
    add_q(down_oth, up_oth)
    gq.relay(far_oth, A, to_peer)
    gq.relay(far_oth, B, to_peer)
    gq.complete(far_oth)
    add_q(far_oth)

    for j in range(2):
        for r in range(2):
            at = slice(r * rows, (r + 1) * rows)
            for ref, base in ((qx, other * 4), (qb.at[0], par * 4)):
                ref[j, at, :] = (rope(acc[1, :, tile(base + 2 * j + r, hd)]) * query_scale).astype(
                    jnp.bfloat16
                )
        send(qx.at[j], qb.at[1, j], q_sem.at[j], to_pair)

    kv_wait(down_oth, 0)
    kv_send(kvb.at[down_oth], down_oth, 0, to_up)
    kv_wait(up_oth, 1)
    kv_send(kvb.at[up_oth], up_oth, 1, to_down)
    kv_wait(down_oth, 1)
    kv_wait(up_oth, 0)

    for i in range(1, SHARDS):
        blk = (ctx + SHARDS - i) % SHARDS
        await_copy(posb.at[blk], pos_sem.at[blk])
    for src, blk in ((0, ctx), (1, pair)):
        col = jnp.transpose(posb[blk])[:, :1]
        for r in range(2):
            qpos[src, r * rows : (r + 1) * rows, :] = col

    def unit(src, j, step, first):
        zr = (z + step + step // 2 - 2 * (step // 3)) % 4
        blocks = pl.ds(zr * 2, 2)
        kk = kvb[blocks, :, tile(j, hd)].reshape(2 * rows, hd)
        vv = kvb[blocks, :, tile(2 + j, hd)].reshape(2 * rows, hd)
        vv = jnp.concatenate([vv, jnp.ones_like(vv)], 1)
        kp = jnp.concatenate([posb[zr * 2, :1, :], posb[zr * 2 + 1, :1, :]], 1)
        s = lax.dot_general(
            qb[src, j], kk, (((1,), (1,)), ((), ())), preferred_element_type=jnp.float32
        )
        w = jnp.exp2(jnp.tanh(s * 0.02) * EXP_SCALE)
        w = jnp.where(kp <= qpos[src], w, 0.0).astype(jnp.bfloat16)
        part = jnp.dot(w, vv, preferred_element_type=jnp.float32)
        num[src, j] = part if first else num[src, j] + part

    def result(src, j, r):
        n = num[src, j, r * rows : (r + 1) * rows, :]
        return (n[:, :hd] / n[:, hd:]).astype(jnp.bfloat16)

    num[...] = jnp.zeros_like(num)

    @pl.loop(0, 2)
    def _(j):
        @pl.loop(0, 3)
        def _(i):
            unit(0, j, i, False)

    for j in range(2):
        await_copy(qb.at[1, j], q_sem.at[j])
        if j == 0:
            for blk in (far_own, far_oth):
                kv_wait(blk, 0)
                kv_wait(blk, 1)

        @pl.loop(0, 4)
        def _(i):
            unit(1, j, i, False)

        for r in range(2):
            osend[2 * j + r] = result(1, j, r)
            send(osend.at[2 * j + r], orecv.at[2 * j + r], o_sem.at[2 * j + r], to_pair)

    @pl.loop(0, 2)
    def _(j):
        unit(0, j, 3, False)

    for j in range(2):
        for r in range(2):
            o_ref[:, tile(par * 4 + 2 * j + r, hd)] = result(0, j, r)
    for h in range(4):
        await_copy(orecv.at[h], o_sem.at[h])
        o_ref[:, tile(other * 4 + h, hd)] = orecv[h]

    for copy in sends:
        copy.wait_send()


def on_device(tokens, token_pos, norm_gain, query_weight, key_weight, value_weight):
    rows, feats = tokens.shape
    depth, nq = query_weight.shape
    nk = key_weight.shape[1]
    half = HEAD_DIM // 2
    freq = 10000.0 ** (-jnp.arange(half, dtype=jnp.float32) * 2.0 / HEAD_DIM)
    position = token_pos.astype(jnp.float32)
    angle = position[:, None] * freq[None, :]
    cosine, sine = jnp.cos(angle), jnp.sin(angle)
    cosine = jnp.concatenate([cosine, cosine], -1)
    sine = jnp.concatenate([-sine, sine], -1)
    vmem = pl.BlockSpec(memory_space=pltpu.VMEM)
    hbm = pl.BlockSpec(memory_space=pl.ANY)
    bf16, f32 = jnp.bfloat16, jnp.float32
    dma = pltpu.SemaphoreType.DMA
    return pl.pallas_call(
        kernel,
        out_shape=jax.ShapeDtypeStruct((rows, nq), bf16),
        in_specs=[hbm, vmem, hbm, hbm, hbm, vmem, vmem, vmem],
        out_specs=vmem,
        scratch_shapes=[
            pltpu.VMEM((rows, feats), bf16),
            pltpu.VMEM((SHARDS, rows, depth), bf16),
            pltpu.VMEM((SHARDS, depth, 2 * nk), bf16),
            pltpu.VMEM((SHARDS, depth, nq), bf16),
            pltpu.VMEM((2, rows, nq), f32),
            pltpu.VMEM((SHARDS, 8, rows), f32),
            pltpu.VMEM((2, 2 * rows, 1), f32),
            pltpu.VMEM((SHARDS, rows, nk), bf16),
            pltpu.VMEM((rows, nk), bf16),
            pltpu.VMEM((2, 2, 2 * rows, HEAD_DIM), bf16),
            pltpu.VMEM((2, 2 * rows, HEAD_DIM), bf16),
            pltpu.VMEM((2, 2, 2 * rows, 2 * HEAD_DIM), f32),
            pltpu.VMEM((4, rows, HEAD_DIM), bf16),
            pltpu.VMEM((4, rows, HEAD_DIM), bf16),
            dma((4,)),
            dma((96,)),
            dma((SHARDS, 4)),
            dma((SHARDS, 4)),
            dma((SHARDS, 2)),
            dma((2,)),
            dma((4,)),
            dma((SHARDS,)),
        ],
        compiler_params=pltpu.CompilerParams(
            collective_id=0, has_side_effects=True, vmem_limit_bytes=62 * 1024 * 1024
        ),
        name="block",
    )(
        tokens, norm_gain.reshape(1, feats), query_weight, key_weight, value_weight,
        cosine, sine, jnp.broadcast_to(position[None, :], (8, rows)),
    )


def solution(mesh):
    in_specs = (
        P(("grp", "ctx"), None),
        P(("grp", "ctx")),
        P(),
        P("ctx", "tp"),
        P("ctx", "tp"),
        P("ctx", "tp"),
    )
    out_specs = P(("grp", "ctx"), "tp")
    return jax.shard_map(
        on_device, mesh=mesh, in_specs=in_specs, out_specs=out_specs, check_vma=False
    )
```

time: 665 us -> 113 us (0.17)
  waiting for transfers between devices: 500 us -> 0 us
  Pallas kernels: 0 us -> 106 us
  matrix products: 62.5 us -> 0 us
  local copies, waits for them, and re-layouts: 49.9 us -> 4.21 us
  blocking collectives: 21.1 us -> 0 us
  between operations: 13.6 us -> 0.02 us
  other arithmetic: 15.7 us -> 2.7 us
    all_gather x2 -> x0, waiting for transfers between devices: 500 us -> none  [side_by_side(): lax.all_gather(both, axis, axis=dim, tiled=True)]
    pallas_call x0 -> x1, Pallas kernels: none -> 106 us  [on_device(): pl.pallas_call(kernel, out_shape=jax.ShapeDtypeStruct((rows, nq), bf16),...]
    dot_general x67 -> x0, matrix products: 62.5 us -> none  [the longest x32 28 us: compute(): jnp.einsum('ngrd,mgd->grnm', query_run, key_part, preferred_element_type=...]
    dynamic_slice x48 -> x0, local copies, waits for them, and re-layouts: 32.5 us -> none  [the longest x16 15.6 us: one_block(): lax.dynamic_slice_in_dim(key_rows, index * width, width, 0)]
    all_gather x1 -> x0, blocking collectives: 21.1 us -> none  [on_device(): lax.all_gather(token_pos, 'ctx', axis=0, tiled=True)]
    div x2 -> x0, local copies, waits for them, and re-layouts: 6.89 us -> none  [on_device(): attended = numerator / jnp.transpose(total, (2, 0, 1))[..., None]]
  transfers between devices with their start and end apart: 2 -> 0, of which waited for: 2 -> 0; matrix products, arithmetic and copies ran while one was open for 2% -> 0% of each run, Pallas kernels for 0% -> 0%
where the time goes in v1:
time: 113 us
  Pallas kernels  106 us (94%)
  local copies, waits for them, and re-layouts  4.21 us (4%)
  other arithmetic  2.7 us (2%)
    pallas_call x1, Pallas kernels, on_device(): pl.pallas_call(kernel, out_shape=jax.ShapeDtypeStruct((rows, nq), bf16),...  106 us
    unnamed x1, local copies, waits for them, and re-layouts  2.26 us

profile of v1, /device:TPU:1, one launch (start us, length us, event | category | flops | bytes accessed | tf_op | source)
XLA Modules:
  0.0 112.7 jit_solution(6539770444877672946)
XLA Ops:
  0.0 0.7 convert_element_type.3
  0.7 0.6 broadcast_in_dim.2.pos_ref
  1.3 1.3 %reshape.11.gain_ref = f32[1,4608]{1,0:T(1,128)} reshape(f32[4608]{0:T(1024)} %param.8) | data formatting | bytes 36864 | tf_op jit(solution)/shard_map/reshape | solution.py:382
  2.6 1.0 fusion
  3.6 1.0 pad_maximum_fusion
  4.7 105.8 %block.1 = bf16[512,1024]{1,0:T(8,128)(2,1)} custom-call(bf16[512,4608]{1,0:T(8,128)(2,1)} %x_hbm.1, f32[1,4608]{1,0:T(1,128)} %reshape.11.gain_ref, bf16[576,1024]{1,0:T(8,128)(2,1)} %wq_hbm.1, bf16[576,512]{1,0:T(8,128)(2,1)} %wk_hbm.1, bf16[576,512]{1,0:T(8,128)(2,1)} %wv_hbm.1, f32[512,128]{1,0:T(8,128)} %get-tuple-element.8.cos_ref, ...), custom_call_target="tpu_custom_call" | custom-call | tf_op jit(solution)/shard_map/block/pallas_call | solution.py:348
  110.4 2.3 %copy.8 = bf16[512,1024]{1,0:T(8,128)(2,1)} copy(bf16[512,1024]{1,0:T(8,128)(2,1)} %block.1) | data formatting | bytes 2097152
  (1 shorter events, 0.0 us)

commit v2 on v1

--- a/solution.py
+++ b/solution.py
@@ -42,7 +42,7 @@
     group = [{"ctx": (ctx + i) % SHARDS} for i in range(1, SHARDS)]
 
     rows, feats = xv.shape
-    depth = wq.shape[1]
+    depth = wkv.shape[1]
     nq, nk = wq_hbm.shape[1], wk_hbm.shape[1]
     hd = HEAD_DIM
     half_rows = rows // 2
@@ -54,7 +54,14 @@
         pltpu.make_async_copy(wk_hbm, wkv.at[ctx, :, pl.ds(0, nk)], local_sem.at[0]),
         pltpu.make_async_copy(wv_hbm, wkv.at[ctx, :, pl.ds(nk, nk)], local_sem.at[1]),
         pltpu.make_async_copy(x_hbm, xv, local_sem.at[2]),
-        pltpu.make_async_copy(wq_hbm, wq.at[ctx], local_sem.at[3]),
+    ] + [
+        pltpu.make_async_copy(
+            wq_hbm.at[:, pl.ds((2 * i + j) * 2 * hd, 2 * hd)],
+            wq.at[j, ctx, :, pl.ds(i * 2 * hd, 2 * hd)],
+            local_sem.at[3 + 2 * i + j],
+        )
+        for i in range(2)
+        for j in range(2)
     ]
     for load in loads:
         load.start()
@@ -111,7 +118,7 @@
     far_own, far_oth = far * 2 + par, far * 2 + other
 
     gkv = Gather(wkv, wkv_sem, SPLIT_KV)
-    gq = Gather(wq, wq_sem, SPLIT_Q)
+    gq = [Gather(wq.at[j], wq_sem.at[j], SPLIT_Q) for j in range(2)]
 
     def add(buf, shard, at, first=False):
         width = 256
@@ -119,16 +126,17 @@
         @pl.loop(0, buf.shape[2] // width)
         def _(j):
             cols = tile(j, width)
+            to = pl.ds(pl.multiple_of(at.start + j * width, width), width)
             part = jnp.dot(normed[shard], buf[shard, :, cols], preferred_element_type=jnp.float32)
-            acc[at, :, cols] = part if first else acc[at, :, cols] + part
+            acc[:, to] = part if first else acc[:, to] + part
 
     def add_kv(*shards, first=False):
         for s in shards:
-            add(wkv, s, 0, first)
-
-    def add_q(*shards, first=False):
+            add(wkv, s, pl.ds(0, 2 * nk), first)
+
+    def add_q(j, *shards, first=False):
         for s in shards:
-            add(wq, s, 1, first)
+            add(wq.at[j], s, pl.ds(2 * nk + j * nk, nk), first)
 
     gkv.send(own, A, to_up, to_pair)
     gkv.send(own, B, to_down, to_cross)
@@ -150,7 +158,9 @@
         for s in range(SHARDS):
             normed[s, at, :] = out[:, s * depth : (s + 1) * depth]
 
-    loads[3].wait()
+    for load in loads[3:]:
+        load.wait()
+    num[...] = jnp.zeros_like(num)
     add_kv(own, first=True)
 
     gkv.relay(down_own, A, to_up, to_pair, to_peer)
@@ -160,12 +170,19 @@
     gkv.complete(pair)
     add_kv(pair)
 
+    def start_z(g):
+        g.send(own, A, to_up)
+        g.send(own, B, to_down)
+        g.send(own, B, to_up)
+        g.send(own, A, to_down)
+
+    def start_y(g):
+        g.send(own, A, to_pair)
+        g.send(own, B, to_cross)
+
     gkv.relay(down_own, B, to_cross, to_peer)
     gkv.relay(up_own, A, to_pair, to_peer)
-    gq.send(own, A, to_up)
-    gq.send(own, B, to_down)
-    gq.send(own, B, to_up)
-    gq.send(own, A, to_down)
+    start_z(gq[0])
     gkv.relay(down_oth, A, to_peer)
     gkv.relay(up_oth, B, to_peer)
     gkv.complete(down_own, up_own)
@@ -173,97 +190,103 @@
 
     gkv.relay(far_own, A, to_pair, to_peer)
     gkv.relay(far_own, B, to_cross, to_peer)
-    gq.send(own, A, to_pair)
-    gq.send(own, B, to_cross)
+    start_y(gq[0])
     gkv.relay(up_oth, A, to_peer)
     gkv.relay(down_oth, B, to_peer)
     gkv.complete(down_oth, up_oth, far_own)
     add_kv(down_oth, up_oth, far_own)
-    add_q(own, first=True)
-
+    add_q(0, own, first=True)
+
+    gq[0].relay(down_own, A, to_up, to_pair, to_peer)
+    gq[0].relay(up_own, B, to_down, to_cross, to_peer)
+    start_z(gq[1])
     gkv.relay(far_oth, A, to_peer)
     gkv.relay(far_oth, B, to_peer)
-    gq.relay(down_own, A, to_up, to_peer)
-    gq.relay(up_own, B, to_down, to_cross, to_peer)
+    gq[0].relay(down_own, B, to_cross, to_peer)
+    gq[0].relay(up_own, A, to_pair, to_peer)
     gkv.complete(far_oth)
     add_kv(far_oth)
 
     def rope(u):
         return u * cos_ref[...] + pltpu.roll(u, hd // 2, 1) * sin_ref[...]
 
-    for h in range(2):
+    for j in range(2):
         for ref, base in ((kvb.at[ctx], par * 2), (kvx, other * 2)):
-            ref[:, h * hd : (h + 1) * hd] = rope(acc[0, :, tile(base + h, hd)]).astype(jnp.bfloat16)
-            ref[:, (2 + h) * hd : (3 + h) * hd] = acc[0, :, tile(nk // hd + base + h, hd)].astype(
-                jnp.bfloat16
+            ref[j, :, :hd] = rope(acc[:, tile(base + j, hd)]).astype(jnp.bfloat16)
+            ref[j, :, hd:] = acc[:, tile(nk // hd + base + j, hd)].astype(jnp.bfloat16)
+
+    def kv_half(blk, j, half):
+        return kvb.at[blk, j, pl.ds(half * half_rows, half_rows), :]
+
+    def kv_send(blk, j, half, *devs):
+        for dev in devs:
+            ref = kv_half(blk, j, half)
+            send(ref, ref, kv_sem.at[blk, j, half], dev)
+
+    def kv_wait(blk, j, half):
+        await_copy(kv_half(blk, j, half), kv_sem.at[blk, j, half])
+
+    def kv_to_pair(j):
+        for half in range(2):
+            send(
+                kvx.at[j, pl.ds(half * half_rows, half_rows), :], kv_half(ctx, j, half),
+                kv_sem.at[ctx, j, half], to_pair,
             )
 
-    def kv_half(ref, half):
-        return ref.at[pl.ds(half * half_rows, half_rows), :]
-
-    def kv_send(src, blk, half, dev):
-        send(kv_half(src, half), kv_half(kvb.at[blk], half), kv_sem.at[blk, half], dev)
-
-    def kv_wait(blk, half):
-        await_copy(kv_half(kvb.at[blk], half), kv_sem.at[blk, half])
-
-    for half in range(2):
-        kv_send(kvx, ctx, half, to_pair)
-    for half in range(2):
-        kv_send(kvb.at[ctx], ctx, half, to_up)
-        kv_send(kvb.at[ctx], ctx, 1 - half, to_down)
-    gq.send(down_own, A, to_pair)
-
-    gq.relay(down_own, B, to_cross, to_peer)
-    gq.relay(up_own, A, to_pair, to_peer)
-    gq.relay(pair, A, to_peer)
-    gq.relay(pair, B, to_peer)
-    gq.complete(down_own, up_own)
-    add_q(down_own, up_own)
-    gq.relay(far_own, A, to_pair, to_peer)
-    gq.relay(far_own, B, to_cross, to_peer)
-    gq.complete(pair)
-    add_q(pair)
-    kv_wait(pair, 0)
-    kv_send(kvb.at[pair], pair, 0, to_up)
-    kv_wait(pair, 1)
-    kv_send(kvb.at[pair], pair, 1, to_down)
-    kv_send(kvb.at[pair], pair, 1, to_up)
-    kv_send(kvb.at[pair], pair, 0, to_down)
-    gq.relay(down_oth, A, to_peer)
-    gq.relay(up_oth, B, to_peer)
-    gq.complete(far_own)
-    add_q(far_own)
-    kv_wait(down_own, 0)
-    kv_send(kvb.at[down_own], down_own, 0, to_up)
-    kv_wait(up_own, 1)
-    kv_send(kvb.at[up_own], up_own, 1, to_down)
-    kv_wait(down_own, 1)
-    kv_wait(up_own, 0)
-    gq.relay(up_oth, A, to_peer)
-    gq.relay(down_oth, B, to_peer)
-    gq.complete(down_oth, up_oth)
-    add_q(down_oth, up_oth)
-    gq.relay(far_oth, A, to_peer)
-    gq.relay(far_oth, B, to_peer)
-    gq.complete(far_oth)
-    add_q(far_oth)
-
-    for j in range(2):
+    def kv_to_z(blk, j):
+        for half in range(2):
+            kv_send(blk, j, half, to_up)
+            kv_send(blk, j, 1 - half, to_down)
+
+    def kv_relay(low, high, j):
+        kv_wait(low, j, 0)
+        kv_send(low, j, 0, to_up)
+        kv_wait(high, j, 1)
+        kv_send(high, j, 1, to_down)
+        kv_wait(low, j, 1)
+        kv_wait(high, j, 0)
+
+    kv_to_pair(0)
+    kv_to_z(ctx, 0)
+    gq[0].relay(far_own, A, to_pair, to_peer)
+    gq[0].relay(far_own, B, to_cross, to_peer)
+    start_y(gq[1])
+    gq[0].relay(pair, A, to_peer)
+    gq[0].relay(pair, B, to_peer)
+    gq[1].relay(down_own, A, to_up, to_pair, to_peer)
+    gq[1].relay(up_own, B, to_down, to_cross, to_peer)
+    gq[0].relay(down_oth, A, to_peer)
+    gq[0].relay(up_oth, B, to_peer)
+    gq[0].complete(pair, down_own, up_own)
+    add_q(0, pair, down_own, up_own)
+    gq[1].relay(down_own, B, to_cross, to_peer)
+    gq[1].relay(up_own, A, to_pair, to_peer)
+    gq[0].relay(up_oth, A, to_peer)
+    gq[0].relay(down_oth, B, to_peer)
+    kv_wait(pair, 0, 0)
+    kv_wait(pair, 0, 1)
+    kv_to_z(pair, 0)
+    kv_to_pair(1)
+    gq[0].complete(down_oth, up_oth, far_own)
+    add_q(0, down_oth, up_oth, far_own)
+    kv_relay(down_own, up_own, 0)
+    kv_to_z(ctx, 1)
+    gq[0].relay(far_oth, A, to_peer)
+    gq[0].relay(far_oth, B, to_peer)
+    gq[0].complete(far_oth)
+    add_q(0, far_oth)
+
+    def query(j):
         for r in range(2):
             at = slice(r * rows, (r + 1) * rows)
-            for ref, base in ((qx, other * 4), (qb.at[0], par * 4)):
-                ref[j, at, :] = (rope(acc[1, :, tile(base + 2 * j + r, hd)]) * query_scale).astype(
-                    jnp.bfloat16
-                )
+            for ref, base in ((qx, other), (qb.at[0], par)):
+                u = acc[:, tile(2 * nk // hd + j * (nk // hd) + base * 2 + r, hd)]
+                ref[j, at, :] = (rope(u) * query_scale).astype(jnp.bfloat16)
         send(qx.at[j], qb.at[1, j], q_sem.at[j], to_pair)
 
-    kv_wait(down_oth, 0)
-    kv_send(kvb.at[down_oth], down_oth, 0, to_up)
-    kv_wait(up_oth, 1)
-    kv_send(kvb.at[up_oth], up_oth, 1, to_down)
-    kv_wait(down_oth, 1)
-    kv_wait(up_oth, 0)
+    query(0)
+    gq[1].relay(far_own, A, to_pair, to_peer)
+    gq[1].relay(far_own, B, to_cross, to_peer)
 
     for i in range(1, SHARDS):
         blk = (ctx + SHARDS - i) % SHARDS
@@ -273,11 +296,11 @@
         for r in range(2):
             qpos[src, r * rows : (r + 1) * rows, :] = col
 
-    def unit(src, j, step, first):
+    def unit(src, j, step):
         zr = (z + step + step // 2 - 2 * (step // 3)) % 4
         blocks = pl.ds(zr * 2, 2)
-        kk = kvb[blocks, :, tile(j, hd)].reshape(2 * rows, hd)
-        vv = kvb[blocks, :, tile(2 + j, hd)].reshape(2 * rows, hd)
+        kk = kvb[blocks, j, :, :hd].reshape(2 * rows, hd)
+        vv = kvb[blocks, j, :, hd:].reshape(2 * rows, hd)
         vv = jnp.concatenate([vv, jnp.ones_like(vv)], 1)
         kp = jnp.concatenate([posb[zr * 2, :1, :], posb[zr * 2 + 1, :1, :]], 1)
         s = lax.dot_general(
@@ -285,39 +308,66 @@
         )
         w = jnp.exp2(jnp.tanh(s * 0.02) * EXP_SCALE)
         w = jnp.where(kp <= qpos[src], w, 0.0).astype(jnp.bfloat16)
-        part = jnp.dot(w, vv, preferred_element_type=jnp.float32)
-        num[src, j] = part if first else num[src, j] + part
+        num[src, j] += jnp.dot(w, vv, preferred_element_type=jnp.float32)
+
+    def units(src, j, first, last):
+        if last - first == 1:
+            unit(src, j, first)
+        else:
+            pl.loop(first, last)(lambda i: unit(src, j, i))
 
     def result(src, j, r):
         n = num[src, j, r * rows : (r + 1) * rows, :]
         return (n[:, :hd] / n[:, hd:]).astype(jnp.bfloat16)
 
-    num[...] = jnp.zeros_like(num)
-
-    @pl.loop(0, 2)
-    def _(j):
-        @pl.loop(0, 3)
-        def _(i):
-            unit(0, j, i, False)
-
-    for j in range(2):
-        await_copy(qb.at[1, j], q_sem.at[j])
-        if j == 0:
-            for blk in (far_own, far_oth):
-                kv_wait(blk, 0)
-                kv_wait(blk, 1)
-
-        @pl.loop(0, 4)
-        def _(i):
-            unit(1, j, i, False)
-
+    def give_back(j):
         for r in range(2):
             osend[2 * j + r] = result(1, j, r)
             send(osend.at[2 * j + r], orecv.at[2 * j + r], o_sem.at[2 * j + r], to_pair)
 
-    @pl.loop(0, 2)
-    def _(j):
-        unit(0, j, 3, False)
+    def far_wait(j):
+        for blk in (far_own, far_oth):
+            kv_wait(blk, j, 0)
+            kv_wait(blk, j, 1)
+
+    units(0, 0, 0, 1)
+    gq[1].relay(pair, A, to_peer)
+    gq[1].relay(pair, B, to_peer)
+    gq[1].relay(down_oth, A, to_peer)
+    gq[1].relay(up_oth, B, to_peer)
+    kv_relay(down_oth, up_oth, 0)
+    units(0, 0, 1, 3)
+    add_q(1, own, first=True)
+    gq[1].complete(pair, down_own, up_own)
+    add_q(1, pair, down_own, up_own)
+    gq[1].relay(up_oth, A, to_peer)
+    gq[1].relay(down_oth, B, to_peer)
+    kv_wait(pair, 1, 0)
+    kv_wait(pair, 1, 1)
+    kv_to_z(pair, 1)
+    gq[1].complete(down_oth, up_oth, far_own)
+    add_q(1, down_oth, up_oth, far_own)
+    await_copy(qb.at[1, 0], q_sem.at[0])
+    units(1, 0, 0, 3)
+    gq[1].relay(far_oth, A, to_peer)
+    gq[1].relay(far_oth, B, to_peer)
+    gq[1].complete(far_oth)
+    add_q(1, far_oth)
+    query(1)
+    far_wait(0)
+    units(1, 0, 3, 4)
+    give_back(0)
+    kv_relay(down_own, up_own, 1)
+    units(0, 0, 3, 4)
+    units(0, 1, 0, 1)
+    kv_relay(down_oth, up_oth, 1)
+    units(0, 1, 1, 3)
+    await_copy(qb.at[1, 1], q_sem.at[1])
+    units(1, 1, 0, 3)
+    far_wait(1)
+    units(1, 1, 3, 4)
+    give_back(1)
+    units(0, 1, 3, 4)
 
     for j in range(2):
         for r in range(2):
@@ -354,22 +404,22 @@
             pltpu.VMEM((rows, feats), bf16),
             pltpu.VMEM((SHARDS, rows, depth), bf16),
             pltpu.VMEM((SHARDS, depth, 2 * nk), bf16),
-            pltpu.VMEM((SHARDS, depth, nq), bf16),
-            pltpu.VMEM((2, rows, nq), f32),
+            pltpu.VMEM((2, SHARDS, depth, nk), bf16),
+            pltpu.VMEM((rows, nq + 2 * nk), f32),
             pltpu.VMEM((SHARDS, 8, rows), f32),
             pltpu.VMEM((2, 2 * rows, 1), f32),
-            pltpu.VMEM((SHARDS, rows, nk), bf16),
-            pltpu.VMEM((rows, nk), bf16),
+            pltpu.VMEM((SHARDS, 2, rows, 2 * HEAD_DIM), bf16),
+            pltpu.VMEM((2, rows, 2 * HEAD_DIM), bf16),
             pltpu.VMEM((2, 2, 2 * rows, HEAD_DIM), bf16),
             pltpu.VMEM((2, 2 * rows, HEAD_DIM), bf16),
             pltpu.VMEM((2, 2, 2 * rows, 2 * HEAD_DIM), f32),
             pltpu.VMEM((4, rows, HEAD_DIM), bf16),
             pltpu.VMEM((4, rows, HEAD_DIM), bf16),
-            dma((4,)),
-            dma((96,)),
+            dma((7,)),
+            dma((136,)),
             dma((SHARDS, 4)),
-            dma((SHARDS, 4)),
-            dma((SHARDS, 2)),
+            dma((2, SHARDS, 4)),
+            dma((SHARDS, 2, 2)),
             dma((2,)),
             dma((4,)),
             dma((SHARDS,)),

time: 113 us -> 112 us (level)
  no operation moved by 1% of the time
where the time goes in v2:
time: 112 us
  Pallas kernels  105 us (94%)
  local copies, waits for them, and re-layouts  4.21 us (4%)
  other arithmetic  2.7 us (2%)
    pallas_call x1, Pallas kernels, on_device(): pl.pallas_call(kernel, out_shape=jax.ShapeDtypeStruct((rows, nq), bf16),...  105 us
    unnamed x1, local copies, waits for them, and re-layouts  2.26 us

profile of v2, /device:TPU:1, one launch (start us, length us, event | category | flops | bytes accessed | tf_op | source)
XLA Modules:
  0.0 112.0 jit_solution(2216327765474265396)
XLA Ops:
  0.0 0.7 convert_element_type.3
  0.7 0.6 broadcast_in_dim.2.pos_ref
  1.3 1.3 %reshape.11.gain_ref = f32[1,4608]{1,0:T(1,128)} reshape(f32[4608]{0:T(1024)} %param.8) | data formatting | bytes 36864 | tf_op jit(solution)/shard_map/reshape | solution.py:432
  2.6 1.0 fusion
  3.6 1.0 pad_maximum_fusion
  4.7 105.0 %block.1 = bf16[512,1024]{1,0:T(8,128)(2,1)} custom-call(bf16[512,4608]{1,0:T(8,128)(2,1)} %x_hbm.1, f32[1,4608]{1,0:T(1,128)} %reshape.11.gain_ref, bf16[576,1024]{1,0:T(8,128)(2,1)} %wq_hbm.1, bf16[576,512]{1,0:T(8,128)(2,1)} %wk_hbm.1, bf16[576,512]{1,0:T(8,128)(2,1)} %wv_hbm.1, f32[512,128]{1,0:T(8,128)} %get-tuple-element.8.cos_ref, ...), custom_call_target="tpu_custom_call" | custom-call | tf_op jit(solution)/shard_map/block/pallas_call | solution.py:398
  109.7 2.3 %copy.8 = bf16[512,1024]{1,0:T(8,128)(2,1)} copy(bf16[512,1024]{1,0:T(8,128)(2,1)} %block.1) | data formatting | bytes 2097152
  (1 shorter events, 0.0 us)

commit v3 on v2

v3 whole, which is shorter than its diff:
```python
import functools
import math

import jax
import jax.numpy as jnp
import numpy as np
from jax import lax
from jax.experimental import pallas as pl
from jax.experimental.pallas import tpu as pltpu
from jax.sharding import PartitionSpec as P

HEAD_DIM = 128
MESH = pl.DeviceIdType.MESH
query_scale = 144.0 ** (-0.5)
EXP_SCALE = 50.0 * math.log2(math.e)
SHARDS = 8
SPLITS = (144, 128, 112, 128)


def tile(index, size):
    return pl.ds(pl.multiple_of(index * size, size), size)


def kernel(
    x_hbm, gain_ref, wq_hbm, wk_hbm, wv_hbm, freq_ref, pos_ref,
    o_ref,
    cos_ref, sin_ref, xv, normed, weights, acc, posb, qpos, kvb, kvx, qb, qx, num, osend, orecv,
    local_sem, send_sem, weight_sem, kv_sem, q_sem, o_sem, pos_sem,
):
    ctx = lax.axis_index("ctx")
    grp = lax.axis_index("grp")
    z, par = ctx // 2, ctx % 2
    y_hi, core = grp // 2, grp % 2
    up, down, far = (z + 1) % 4, (z + 3) % 4, (z + 2) % 4
    other = 1 - par
    pair = z * 2 + other
    to_up = {"ctx": up * 2 + par}
    to_down = {"ctx": down * 2 + par}
    to_pair = {"ctx": pair}
    to_cross = {"ctx": pair, "grp": (1 - y_hi) * 2 + core}
    to_peer = {"grp": y_hi * 2 + (1 - core)}
    group = [{"ctx": (ctx + i) % SHARDS} for i in range(1, SHARDS)]

    rows, feats = xv.shape
    depth = weights.shape[2]
    nq, nk = wq_hbm.shape[1], wk_hbm.shape[1]
    hd = HEAD_DIM
    half_rows = rows // 2

    barrier = pltpu.get_barrier_semaphore()
    for dev in group + [to_cross, to_peer]:
        pl.semaphore_signal(barrier, inc=1, device_id=dev, device_id_type=MESH)
    loads = []

    def load(src, dst):
        loads.append(pltpu.make_async_copy(src, dst, local_sem.at[len(loads)]))

    for j in range(2):
        for i in range(2):
            for at, ref in ((i, wk_hbm), (2 + i, wv_hbm)):
                load(
                    ref.at[:, pl.ds((2 * i + j) * hd, hd)],
                    weights.at[j, ctx, :, pl.ds(at * hd, hd)],
                )
    for j in range(2):
        for i in range(2):
            load(
                wq_hbm.at[:, pl.ds((2 * i + j) * 2 * hd, 2 * hd)],
                weights.at[2 + j, ctx, :, pl.ds(i * 2 * hd, 2 * hd)],
            )
    load(x_hbm, xv)
    for item in loads[:8] + loads[-1:] + loads[8:-1]:
        item.start()
    for item in loads[:4]:
        item.wait()
    pl.semaphore_wait(barrier, SHARDS + 1)

    sends = []

    def copy_of(src, dst, recv, dev, at):
        return pltpu.make_async_remote_copy(
            src_ref=src, dst_ref=dst, send_sem=send_sem.at[at], recv_sem=recv,
            device_id=dev, device_id_type=MESH,
        )

    def send(src, dst, recv, dev):
        copy = copy_of(src, dst, recv, dev, len(sends))
        copy.start()
        sends.append(copy)

    def await_copy(dst, recv):
        copy_of(dst, dst, recv, to_peer, 0).wait_recv()

    class Gather:
        def __init__(self, buf, sem, split):
            self.buf, self.sem, self.split = buf, sem, split

        def piece(self, shard, owner, kind):
            base = owner * (depth // 2) + (self.split if kind else 0)
            size = depth // 2 - self.split if kind else self.split
            return self.buf.at[shard, pl.ds(pl.multiple_of(base, 16), size), :]

        def send(self, shard, kind, *devs):
            ref = self.piece(shard, core, kind)
            for dev in devs:
                send(ref, ref, self.sem.at[shard, core * 2 + kind], dev)

        def wait(self, shard, kind, owner=core):
            await_copy(self.piece(shard, owner, kind), self.sem.at[shard, owner * 2 + kind])

        def relay(self, shard, kind, *devs):
            self.wait(shard, kind)
            self.send(shard, kind, *devs)

        def complete(self, *shards):
            for s in shards:
                self.wait(s, 0, 1 - core)
                self.wait(s, 1, 1 - core)

    A, B = 0, 1
    own = ctx
    up_own, up_oth = up * 2 + par, up * 2 + other
    down_own, down_oth = down * 2 + par, down * 2 + other
    far_own, far_oth = far * 2 + par, far * 2 + other

    g = [Gather(weights.at[p], weight_sem.at[p], SPLITS[p]) for p in range(4)]

    def add(p, *shards, first=False):
        width = 256

        @pl.loop(0, nk // width)
        def _(i):
            cols = tile(i, width)
            part = sum(
                jnp.dot(normed[s], weights[p, s, :, cols], preferred_element_type=jnp.float32)
                for s in shards
            )
            acc[p, :, cols] = part if first else acc[p, :, cols] + part

    def a1(p):
        g[p].relay(down_own, A, to_up, to_pair, to_peer)
        g[p].relay(up_own, B, to_down, to_cross, to_peer)

    def a2(p):
        g[p].relay(down_own, B, to_cross, to_peer)
        g[p].relay(up_own, A, to_pair, to_peer)

    def a3(p):
        g[p].relay(far_own, A, to_pair, to_peer)
        g[p].relay(far_own, B, to_cross, to_peer)

    def y0(p):
        g[p].relay(pair, A, to_peer)
        g[p].relay(pair, B, to_peer)

    def y1(p):
        g[p].relay(down_oth, A, to_peer)
        g[p].relay(up_oth, B, to_peer)

    def y2(p):
        g[p].relay(up_oth, A, to_peer)
        g[p].relay(down_oth, B, to_peer)

    def y3(p):
        g[p].relay(far_oth, A, to_peer)
        g[p].relay(far_oth, B, to_peer)

    def start_z(p):
        g[p].send(own, A, to_up)
        g[p].send(own, B, to_down)
        g[p].send(own, B, to_up)
        g[p].send(own, A, to_down)

    def start_y(p):
        g[p].send(own, A, to_pair)
        g[p].send(own, B, to_cross)

    def finish(p, *shards):
        g[p].complete(*shards)
        add(p, *shards)

    start_z(0)
    start_y(0)
    posb[ctx] = jnp.broadcast_to(pos_ref[...].reshape(1, rows), (8, rows)).astype(jnp.float32)
    for item in loads[4:8]:
        item.wait()
    start_y(1)

    loads[-1].wait()
    block = 64
    gain = gain_ref[...].reshape(1, feats)

    @pl.loop(0, rows // block)
    def _(i):
        at = tile(i, block)
        value = xv[at, :].astype(jnp.float32)
        scale = lax.rsqrt(jnp.mean(value * value, -1, keepdims=True) + 1e-06)
        out = (value * scale * gain).astype(jnp.bfloat16)
        for s in range(SHARDS):
            normed[s, at, :] = out[:, s * depth : (s + 1) * depth]

    for item in loads[8:-1]:
        item.wait()

    def angles():
        angle = jnp.transpose(posb[ctx])[:, :1] * freq_ref[...]
        k = jnp.floor(angle * (2.0 / math.pi) + 0.5)
        t = angle - k * 1.5703125
        t = t - k * 4.8375129699707031e-4
        t = t - k * 7.5497899548918822e-8
        q = k - 4.0 * jnp.floor(k * 0.25)
        s = t * t
        sin = t + t * s * (-1.6666654611e-1 + s * (8.3321608736e-3 - s * 1.9515295891e-4))
        cos = 1.0 - 0.5 * s + s * s * (
            4.166664568298827e-2 + s * (s * 2.443315711809948e-5 - 1.388731625493765e-3)
        )
        odd = (q == 1.0) | (q == 3.0)
        sine = jnp.where(odd, cos, sin)
        cosine = jnp.where(odd, sin, cos)
        lane = lax.broadcasted_iota(jnp.int32, sine.shape, 1)
        sin_ref[...] = jnp.where((q >= 2.0) ^ (lane < hd // 2), -sine, sine)
        cos_ref[...] = jnp.where((q == 1.0) | (q == 2.0), -cosine, cosine)

    def rope(u):
        return u * cos_ref[...] + pltpu.roll(u, hd // 2, 1) * sin_ref[...]

    def keys_values(j):
        for ref, base in ((kvb.at[ctx], par), (kvx, other)):
            ref[j, :, :hd] = rope(acc[j, :, tile(base, hd)]).astype(jnp.bfloat16)
            ref[j, :, hd:] = acc[j, :, tile(2 + base, hd)].astype(jnp.bfloat16)

    def query(j):
        for r in range(2):
            at = slice(r * rows, (r + 1) * rows)
            for ref, base in ((qx, other), (qb.at[0], par)):
                u = acc[2 + j, :, tile(base * 2 + r, hd)]
                ref[j, at, :] = (rope(u) * query_scale).astype(jnp.bfloat16)
            send(qx.at[j, at, :], qb.at[1, j, at, :], q_sem.at[j, r], to_pair)

    def query_wait(j, r):
        at = slice(r * rows, (r + 1) * rows)
        await_copy(qb.at[1, j, at, :], q_sem.at[j, r])

    def kv_half(blk, j, half):
        return kvb.at[blk, j, pl.ds(half * half_rows, half_rows), :]

    def kv_send(blk, j, half, *devs):
        for dev in devs:
            ref = kv_half(blk, j, half)
            send(ref, ref, kv_sem.at[blk, j, half], dev)

    def kv_wait(blk, j, half):
        await_copy(kv_half(blk, j, half), kv_sem.at[blk, j, half])

    def kv_to_pair(j):
        for half in range(2):
            send(
                kvx.at[j, pl.ds(half * half_rows, half_rows), :], kv_half(ctx, j, half),
                kv_sem.at[ctx, j, half], to_pair,
            )

    def kv_to_z(blk, j):
        for half in range(2):
            kv_send(blk, j, half, to_up)
            kv_send(blk, j, 1 - half, to_down)

    def kv_pair(j):
        kv_wait(pair, j, 0)
        kv_wait(pair, j, 1)
        kv_to_z(pair, j)

    def kv_relay(low, high, j):
        kv_wait(low, j, 0)
        kv_send(low, j, 0, to_up)
        kv_wait(high, j, 1)
        kv_send(high, j, 1, to_down)
        kv_wait(low, j, 1)
        kv_wait(high, j, 0)

    def unit(src, j, step, at=slice(None)):
        zr = (z + step + step // 2 - 2 * (step // 3)) % 4
        blocks = pl.ds(zr * 2, 2)
        kk = kvb[blocks, j, :, :hd].reshape(2 * rows, hd)
        vv = kvb[blocks, j, :, hd:].reshape(2 * rows, hd)
        vv = jnp.concatenate([vv, jnp.ones_like(vv)], 1)
        kp = jnp.concatenate([posb[zr * 2, :1, :], posb[zr * 2 + 1, :1, :]], 1)
        s = lax.dot_general(
            qb[src, j, at, :], kk, (((1,), (1,)), ((), ())), preferred_element_type=jnp.float32
        )
        w = jnp.exp2(jnp.tanh(s * 0.02) * EXP_SCALE)
        w = jnp.where(kp <= qpos[src, at, :], w, 0.0).astype(jnp.bfloat16)
        num[src, j, at, :] += jnp.dot(w, vv, preferred_element_type=jnp.float32)

    def units(src, j, first, last):
        if last - first == 1:
            unit(src, j, first)
        else:
            pl.loop(first, last)(lambda i: unit(src, j, i))

    halves = [slice(r * rows, (r + 1) * rows) for r in range(2)]

    def result(src, j, r):
        n = num[src, j, r * rows : (r + 1) * rows, :]
        return (n[:, :hd] / n[:, hd:]).astype(jnp.bfloat16)

    def give_back(j, r):
        osend[2 * j + r] = result(1, j, r)
        send(osend.at[2 * j + r], orecv.at[2 * j + r], o_sem.at[2 * j + r], to_pair)

    def far_wait(j):
        for blk in (far_own, far_oth):
            kv_wait(blk, j, 0)
            kv_wait(blk, j, 1)

    add(0, own, first=True)
    for dev in group:
        send(posb.at[ctx], posb.at[ctx], pos_sem.at[ctx], dev)
    angles()
    a1(0)
    start_z(1)
    y0(0)
    num[...] = jnp.zeros_like(num)
    a2(0)
    y0(1)
    finish(0, pair)
    a3(0)
    y1(0)
    finish(0, down_own, up_own)
    a1(1)
    start_z(2)
    y2(0)
    add(1, own, first=True)
    finish(1, pair)
    a2(1)
    y3(0)
    finish(0, down_oth, up_oth, far_own)
    finish(0, far_oth)
    keys_values(0)
    kv_to_pair(0)
    a3(1)
    y1(1)
    start_y(2)
    finish(1, down_own, up_own)
    a1(2)
    start_z(3)
    kv_to_z(ctx, 0)
    y2(1)
    add(2, own, first=True)
    a2(2)
    for i in range(1, SHARDS):
        blk = (ctx + SHARDS - i) % SHARDS
        await_copy(posb.at[blk], pos_sem.at[blk])
    for src, blk in ((0, ctx), (1, pair)):
        col = jnp.transpose(posb[blk])[:, :1]
        for r in range(2):
            qpos[src, r * rows : (r + 1) * rows, :] = col
    finish(1, down_oth, up_oth, far_own)
    a3(2)
    start_y(3)
    y3(1)
    finish(1, far_oth)
    keys_values(1)
    a1(3)
    kv_pair(0)
    y0(2)
    a2(3)
    y1(2)
    finish(2, pair, down_own, up_own)
    y2(2)
    kv_relay(down_own, up_own, 0)
    finish(2, down_oth, up_oth, far_own)
    y3(2)
    finish(2, far_oth)
    query(0)
    a3(3)
    units(0, 0, 0, 1)
    y0(3)
    y1(3)
    kv_to_pair(1)
    add(3, own, first=True)
    finish(3, pair, down_own, up_own)
    kv_relay(down_oth, up_oth, 0)
    kv_to_z(ctx, 1)
    y2(3)
    units(0, 0, 1, 3)
    query_wait(0, 0)
    query_wait(0, 1)
    units(1, 0, 0, 1)
    kv_pair(1)
    y3(3)
    finish(3, down_oth, up_oth, far_own)
    units(1, 0, 1, 2)
    finish(3, far_oth)
    query(1)
    units(1, 0, 2, 3)
    far_wait(0)
    units(1, 0, 3, 4)
    give_back(0, 0)
    give_back(0, 1)
    kv_relay(down_own, up_own, 1)
    units(0, 0, 3, 4)
    units(0, 1, 0, 1)
    kv_relay(down_oth, up_oth, 1)
    units(0, 1, 1, 3)
    for r in range(2):
        query_wait(1, r)
        unit(1, 1, 0, halves[r])
    units(1, 1, 1, 3)
    far_wait(1)
    for r in range(2):
        unit(1, 1, 3, halves[r])
        give_back(1, r)
    units(0, 1, 3, 4)

    for j in range(2):
        for r in range(2):
            o_ref[:, tile(par * 4 + 2 * j + r, hd)] = result(0, j, r)
    for h in range(4):
        await_copy(orecv.at[h], o_sem.at[h])
        o_ref[:, tile(other * 4 + h, hd)] = orecv[h]

    for copy in sends:
        copy.wait_send()


def on_device(tokens, token_pos, norm_gain, query_weight, key_weight, value_weight):
    rows, feats = tokens.shape
    depth, nq = query_weight.shape
    nk = key_weight.shape[1]
    half = HEAD_DIM // 2
    freq = (10000.0 ** (-np.arange(half) * 2.0 / HEAD_DIM)).astype(np.float32)
    freq = jnp.asarray(np.concatenate([freq, freq])[None, :])
    vmem = pl.BlockSpec(memory_space=pltpu.VMEM)
    hbm = pl.BlockSpec(memory_space=pl.ANY)
    bf16, f32 = jnp.bfloat16, jnp.float32
    dma = pltpu.SemaphoreType.DMA
    return pl.pallas_call(
        kernel,
        out_shape=jax.ShapeDtypeStruct((rows, nq), bf16),
        in_specs=[hbm, vmem, hbm, hbm, hbm, vmem, vmem],
        out_specs=vmem,
        scratch_shapes=[
            pltpu.VMEM((rows, HEAD_DIM), f32),
            pltpu.VMEM((rows, HEAD_DIM), f32),
            pltpu.VMEM((rows, feats), bf16),
            pltpu.VMEM((SHARDS, rows, depth), bf16),
            pltpu.VMEM((4, SHARDS, depth, nk), bf16),
            pltpu.VMEM((4, rows, nk), f32),
            pltpu.VMEM((SHARDS, 8, rows), f32),
            pltpu.VMEM((2, 2 * rows, 1), f32),
            pltpu.VMEM((SHARDS, 2, rows, 2 * HEAD_DIM), bf16),
            pltpu.VMEM((2, rows, 2 * HEAD_DIM), bf16),
            pltpu.VMEM((2, 2, 2 * rows, HEAD_DIM), bf16),
            pltpu.VMEM((2, 2 * rows, HEAD_DIM), bf16),
            pltpu.VMEM((2, 2, 2 * rows, 2 * HEAD_DIM), f32),
            pltpu.VMEM((4, rows, HEAD_DIM), bf16),
            pltpu.VMEM((4, rows, HEAD_DIM), bf16),
            dma((13,)),
            dma((160,)),
            dma((4, SHARDS, 4)),
            dma((SHARDS, 2, 2)),
            dma((2, 2)),
            dma((4,)),
            dma((SHARDS,)),
        ],
        compiler_params=pltpu.CompilerParams(
            collective_id=0, has_side_effects=True, vmem_limit_bytes=62 * 1024 * 1024
        ),
        name="block",
    )(
        tokens, norm_gain, query_weight, key_weight, value_weight, freq, token_pos,
    )


def solution(mesh):
    in_specs = (
        P(("grp", "ctx"), None),
        P(("grp", "ctx")),
        P(),
        P("ctx", "tp"),
        P("ctx", "tp"),
        P("ctx", "tp"),
    )
    out_specs = P(("grp", "ctx"), "tp")
    return jax.shard_map(
        on_device, mesh=mesh, in_specs=in_specs, out_specs=out_specs, check_vma=False
    )
```

time: 112 us -> 104 us (0.929)
  Pallas kernels: 105 us -> 102 us
  other arithmetic: 2.7 us -> 0 us
  local copies, waits for them, and re-layouts: 4.21 us -> 2.26 us
    pallas_call x1, Pallas kernels: 105 us -> 102 us  [on_device(): pl.pallas_call(kernel, out_shape=jax.ShapeDtypeStruct((rows, nq), bf16),...]
    reshape x1 -> x0, local copies, waits for them, and re-layouts: 1.34 us -> none  [on_device(): norm_gain.reshape(1, feats)]
where the time goes in v3:
time: 104 us
  Pallas kernels  102 us (98%)
  local copies, waits for them, and re-layouts  2.26 us (2%)
    pallas_call x1, Pallas kernels, on_device(): pl.pallas_call(kernel, out_shape=jax.ShapeDtypeStruct((rows, nq), bf16),...  102 us
    unnamed x1, local copies, waits for them, and re-layouts  2.26 us

profile of v3, /device:TPU:1, one launch (start us, length us, event | category | flops | bytes accessed | tf_op | source)
XLA Modules:
  0.0 104.3 jit_solution(5280447882166086151)
XLA Ops:
  0.0 102.0 %block.1 = bf16[512,1024]{1,0:T(8,128)(2,1)} custom-call(bf16[512,4608]{1,0:T(8,128)(2,1)} %x_hbm.1, f32[4608]{0:T(1024)} %gain_ref.1, bf16[576,1024]{1,0:T(8,128)(2,1)} %wq_hbm.1, bf16[576,512]{1,0:T(8,128)(2,1)} %wk_hbm.1, bf16[576,512]{1,0:T(8,128)(2,1)} %wv_hbm.1, f32[1,128]{1,0:T(1,128)} %constant.2.clone.freq_ref, s32[512]{0:T(512)} %pos_ref.1), custom_call_target="tpu_custom_call" | custom-call | tf_op jit(solution)/shard_map/block/pallas_call | solution.py:437
  102.0 2.3 %copy.9 = bf16[512,1024]{1,0:T(8,128)(2,1)} copy(bf16[512,1024]{1,0:T(8,128)(2,1)} %block.1) | data formatting | bytes 2097152

commit v4 on v3

v4 whole, which is shorter than its diff:
```python
import functools
import math

import jax
import jax.numpy as jnp
import numpy as np
from jax import lax
from jax.experimental import pallas as pl
from jax.experimental.pallas import tpu as pltpu
from jax.sharding import PartitionSpec as P

HEAD_DIM = 128
MESH = pl.DeviceIdType.MESH
query_scale = 144.0 ** (-0.5)
EXP_SCALE = 50.0 * math.log2(math.e)
SHARDS = 8
SENDS = 32
SPLITS = (144, 128, 112, 128)


def tile(index, size):
    return pl.ds(pl.multiple_of(index * size, size), size)


def kernel(
    x_hbm, gain_hbm, wq_hbm, wk_hbm, wv_hbm, freq_hbm, pos_hbm,
    o_hbm,
    gain_ref, freq_ref, pos_ref, cos_ref, sin_ref, xv, normed, weights, acc, posb, qpos, kvb, kvx, qb, qx, num, oown, osend,
    local_sem, out_sem, send_sem, weight_sem, kv_sem, q_sem, o_sem, pos_sem,
):
    ctx = lax.axis_index("ctx")
    grp = lax.axis_index("grp")
    z, par = ctx // 2, ctx % 2
    y_hi, core = grp // 2, grp % 2
    up, down, far = (z + 1) % 4, (z + 3) % 4, (z + 2) % 4
    other = 1 - par
    pair = z * 2 + other
    to_up = {"ctx": up * 2 + par}
    to_down = {"ctx": down * 2 + par}
    to_pair = {"ctx": pair}
    to_cross = {"ctx": pair, "grp": (1 - y_hi) * 2 + core}
    to_peer = {"grp": y_hi * 2 + (1 - core)}
    group = [{"ctx": (ctx + i) % SHARDS} for i in range(1, SHARDS)]

    rows, feats = xv.shape
    depth = weights.shape[2]
    nq, nk = wq_hbm.shape[1], wk_hbm.shape[1]
    hd = HEAD_DIM
    half_rows = rows // 2

    barrier = pltpu.get_barrier_semaphore()
    for dev in group + [to_cross, to_peer]:
        pl.semaphore_signal(barrier, inc=1, device_id=dev, device_id_type=MESH)
    def load(src, dst, at):
        pltpu.make_async_copy(src, dst, local_sem.at[at]).start()

    def loaded(dst, at):
        pltpu.make_async_copy(dst, dst, local_sem.at[at]).wait()

    def load_kv(j):
        for i in range(2):
            for at, ref in ((i, wk_hbm), (2 + i, wv_hbm)):
                load(
                    ref.at[:, pl.ds((2 * i + j) * hd, hd)],
                    weights.at[j, ctx, :, pl.ds(at * hd, hd)],
                    j,
                )

    load_kv(0)
    load(x_hbm, xv, 4)
    load(gain_hbm, gain_ref, 5)
    load(pos_hbm, pos_ref, 6)
    load(freq_hbm, freq_ref, 7)
    load_kv(1)
    for j in range(2):
        for i in range(2):
            load(
                wq_hbm.at[:, pl.ds((2 * i + j) * 2 * hd, 2 * hd)],
                weights.at[2 + j, ctx, :, pl.ds(i * 2 * hd, 2 * hd)],
                2 + j,
            )
    loaded(weights.at[0, ctx], 0)
    pl.semaphore_wait(barrier, SHARDS + 1)

    sends = []

    def copy_of(src, dst, recv, dev, at):
        return pltpu.make_async_remote_copy(
            src_ref=src, dst_ref=dst, send_sem=send_sem.at[at % SENDS], recv_sem=recv,
            device_id=dev, device_id_type=MESH,
        )

    def send(src, dst, recv, dev):
        if len(sends) >= SENDS:
            sends[-SENDS].wait_send()
        copy = copy_of(src, dst, recv, dev, len(sends))
        copy.start()
        sends.append(copy)

    def await_copy(dst, recv):
        copy_of(dst, dst, recv, to_peer, 0).wait_recv()

    A, B = 0, 1
    own = ctx
    up_own, up_oth = up * 2 + par, up * 2 + other
    down_own, down_oth = down * 2 + par, down * 2 + other
    far_own, far_oth = far * 2 + par, far * 2 + other

    def add(p, *shards, first=False):
        width = 256

        @pl.loop(0, nk // width)
        def _(i):
            cols = tile(i, width)
            part = sum(
                jnp.dot(normed[s], weights[p, s, :, cols], preferred_element_type=jnp.float32)
                for s in shards
            )
            acc[p, :, cols] = part if first else acc[p, :, cols] + part

    DN, UP, FAR, PAIR, DNO, UPO, FARO, PEER = 0, 2, 4, 5, 6, 7, 8, 9
    peer_role = [(down_own, 0), (up_own, 1), (far_own, 2), (pair, 3)]
    peer_role += [(down_oth, 4), (up_oth, 5), (far_oth, 6)]

    def part(p, shard, kind):
        base = core * (depth // 2) + (SPLITS[p] if kind else 0)
        size = depth // 2 - SPLITS[p] if kind else SPLITS[p]
        return weights.at[p, shard, pl.ds(pl.multiple_of(base, 16), size), :]

    def side(p, shard, owner):
        return weights.at[p, shard, pl.ds(pl.multiple_of(owner * (depth // 2), 16), depth // 2), :]

    def send_part(p, shard, kind, role, dev):
        ref = part(p, shard, kind)
        send(ref, ref, weight_sem.at[p, role], dev)

    def to_other_core(p, at):
        shard, role = peer_role[at]
        ref = side(p, shard, core)
        send(ref, ref, weight_sem.at[p, PEER + role], to_peer)

    def wait_part(p, shard, kind, role):
        await_copy(part(p, shard, kind), weight_sem.at[p, role])

    def wait_side(p, shard, role):
        await_copy(side(p, shard, core), weight_sem.at[p, role])

    def a1(p):
        wait_part(p, down_own, A, DN + A)
        send_part(p, down_own, A, FAR, to_up)
        send_part(p, down_own, A, DNO, to_pair)
        wait_part(p, up_own, B, UP + B)
        send_part(p, up_own, B, FAR, to_down)
        send_part(p, up_own, B, UPO, to_cross)

    def a2(p):
        wait_part(p, down_own, B, DN + B)
        send_part(p, down_own, B, DNO, to_cross)
        to_other_core(p, 0)
        wait_part(p, up_own, A, UP + A)
        send_part(p, up_own, A, UPO, to_pair)
        to_other_core(p, 1)

    def a3(p):
        wait_side(p, far_own, FAR)
        send_part(p, far_own, A, FARO, to_pair)
        send_part(p, far_own, B, FARO, to_cross)
        to_other_core(p, 2)

    def y0(p):
        wait_side(p, pair, PAIR)
        to_other_core(p, 3)

    def y2(p):
        wait_side(p, down_oth, DNO)
        to_other_core(p, 4)
        wait_side(p, up_oth, UPO)
        to_other_core(p, 5)

    def y3(p):
        wait_side(p, far_oth, FARO)
        to_other_core(p, 6)

    def start_z(p):
        send_part(p, own, A, DN + A, to_up)
        send_part(p, own, B, UP + B, to_down)
        send_part(p, own, B, DN + B, to_up)
        send_part(p, own, A, UP + A, to_down)

    def start_y(p):
        send_part(p, own, A, PAIR, to_pair)
        send_part(p, own, B, PAIR, to_cross)

    def finish(p, *at):
        for i in at:
            shard, role = peer_role[i]
            await_copy(side(p, shard, 1 - core), weight_sem.at[p, PEER + role])
        add(p, *[peer_role[i][0] for i in at])

    dn_, up_, far_, pair_, dno_, upo_, faro_ = range(7)

    start_z(0)
    start_y(0)
    loaded(pos_ref, 6)
    posb[ctx] = jnp.broadcast_to(pos_ref[...].reshape(1, rows), (8, rows)).astype(jnp.float32)
    loaded(weights.at[1, ctx], 1)
    start_y(1)

    loaded(xv, 4)
    loaded(gain_ref, 5)
    loaded(freq_ref, 7)
    block = 64
    gain = gain_ref[...].reshape(1, feats)

    @pl.loop(0, rows // block)
    def _(i):
        at = tile(i, block)
        value = xv[at, :].astype(jnp.float32)
        scale = lax.rsqrt(jnp.mean(value * value, -1, keepdims=True) + 1e-06)
        out = (value * scale * gain).astype(jnp.bfloat16)
        for s in range(SHARDS):
            normed[s, at, :] = out[:, s * depth : (s + 1) * depth]

    loaded(weights.at[2, ctx], 2)
    loaded(weights.at[3, ctx], 3)

    def angles():
        angle = jnp.transpose(posb[ctx])[:, :1] * freq_ref[...]
        k = jnp.floor(angle * (2.0 / math.pi) + 0.5)
        t = angle - k * 1.5703125
        t = t - k * 4.8375129699707031e-4
        t = t - k * 7.5497899548918822e-8
        q = k - 4.0 * jnp.floor(k * 0.25)
        s = t * t
        sin = t + t * s * (-1.6666654611e-1 + s * (8.3321608736e-3 - s * 1.9515295891e-4))
        cos = 1.0 - 0.5 * s + s * s * (
            4.166664568298827e-2 + s * (s * 2.443315711809948e-5 - 1.388731625493765e-3)
        )
        odd = (q == 1.0) | (q == 3.0)
        sine = jnp.where(odd, cos, sin)
        cosine = jnp.where(odd, sin, cos)
        lane = lax.broadcasted_iota(jnp.int32, sine.shape, 1)
        sin_ref[...] = jnp.where((q >= 2.0) ^ (lane < hd // 2), -sine, sine)
        cos_ref[...] = jnp.where((q == 1.0) | (q == 2.0), -cosine, cosine)

    def rope(u):
        return u * cos_ref[...] + pltpu.roll(u, hd // 2, 1) * sin_ref[...]

    def keys_values(j):
        for ref, base in ((kvb.at[ctx], par), (kvx, other)):
            ref[j, :, :hd] = rope(acc[j, :, tile(base, hd)]).astype(jnp.bfloat16)
            ref[j, :, hd:] = acc[j, :, tile(2 + base, hd)].astype(jnp.bfloat16)

    def query(j):
        for r in range(2):
            at = slice(r * rows, (r + 1) * rows)
            for ref, base in ((qx, other), (qb.at[0], par)):
                u = acc[2 + j, :, tile(base * 2 + r, hd)]
                ref[j, at, :] = (rope(u) * query_scale).astype(jnp.bfloat16)
            send(qx.at[j, at, :], qb.at[1, j, at, :], q_sem.at[j, r], to_pair)

    def query_wait(j, r):
        at = slice(r * rows, (r + 1) * rows)
        await_copy(qb.at[1, j, at, :], q_sem.at[j, r])

    def kv_half(blk, j, half):
        return kvb.at[blk, j, pl.ds(half * half_rows, half_rows), :]

    def kv_send(blk, j, half, role, dev):
        ref = kv_half(blk, j, half)
        send(ref, ref, kv_sem.at[j, role], dev)

    def kv_to_pair(j):
        send(kvx.at[j], kvb.at[ctx, j], kv_sem.at[j, 0], to_pair)

    def kv_to_z(blk, j, base):
        for half in range(2):
            kv_send(blk, j, half, base + half, to_up)
            kv_send(blk, j, 1 - half, base + 2 + 1 - half, to_down)

    def kv_pair(j):
        await_copy(kvb.at[pair, j], kv_sem.at[j, 0])
        kv_to_z(pair, j, 6)

    def kv_relay(low, high, j, base):
        await_copy(kv_half(low, j, 0), kv_sem.at[j, base])
        kv_send(low, j, 0, base + 4, to_up)
        await_copy(kv_half(high, j, 1), kv_sem.at[j, base + 3])
        kv_send(high, j, 1, base + 4, to_down)
        await_copy(kv_half(low, j, 1), kv_sem.at[j, base + 1])
        await_copy(kv_half(high, j, 0), kv_sem.at[j, base + 2])

    def unit(src, j, step, at=slice(None)):
        zr = (z + step + step // 2 - 2 * (step // 3)) % 4
        blocks = pl.ds(zr * 2, 2)
        kk = kvb[blocks, j, :, :hd].reshape(2 * rows, hd)
        vv = kvb[blocks, j, :, hd:].reshape(2 * rows, hd)
        vv = jnp.concatenate([vv, jnp.ones_like(vv)], 1)
        kp = jnp.concatenate([posb[zr * 2, :1, :], posb[zr * 2 + 1, :1, :]], 1)
        s = lax.dot_general(
            qb[src, j, at, :], kk, (((1,), (1,)), ((), ())), preferred_element_type=jnp.float32
        )
        w = jnp.exp2(jnp.tanh(s * 0.02) * EXP_SCALE)
        w = jnp.where(kp <= qpos[src, at, :], w, 0.0).astype(jnp.bfloat16)
        num[src, j, at, :] += jnp.dot(w, vv, preferred_element_type=jnp.float32)

    def units(src, j, first, last):
        if last - first == 1:
            unit(src, j, first)
        else:
            pl.loop(first, last)(lambda i: unit(src, j, i))

    halves = [slice(r * rows, (r + 1) * rows) for r in range(2)]

    def result(src, j, r):
        n = num[src, j, r * rows : (r + 1) * rows, :]
        return (n[:, :hd] / n[:, hd:]).astype(jnp.bfloat16)

    def columns(base, h):
        return o_hbm.at[:, tile(base * 4 + h, hd)]

    def give_back(j, r):
        h = 2 * j + r
        osend[h] = result(1, j, r)
        send(osend.at[h], columns(par, h), o_sem.at[0], to_pair)

    def keep(j, r):
        h = 2 * j + r
        oown[h] = result(0, j, r)
        pltpu.make_async_copy(oown.at[h], columns(par, h), out_sem.at[0]).start()

    def far_wait(j):
        await_copy(kvb.at[far_own, j], kv_sem.at[j, 5])
        await_copy(kvb.at[far_oth, j], kv_sem.at[j, 10])

    add(0, own, first=True)
    for dev in group:
        send(posb.at[ctx], posb.at[ctx], pos_sem.at[0], dev)
    angles()
    a1(0)
    start_z(1)
    y0(0)
    num[...] = jnp.zeros_like(num)
    a2(0)
    y0(1)
    finish(0, pair_)
    a3(0)
    finish(0, dn_, up_)
    a1(1)
    start_z(2)
    y2(0)
    add(1, own, first=True)
    finish(1, pair_)
    a2(1)
    y3(0)
    finish(0, dno_, upo_, far_)
    finish(0, faro_)
    keys_values(0)
    kv_to_pair(0)
    a3(1)
    start_y(2)
    finish(1, dn_, up_)
    a1(2)
    start_z(3)
    kv_to_z(ctx, 0, 1)
    y2(1)
    add(2, own, first=True)
    a2(2)
    await_copy(posb.at[pl.ds(0, SHARDS - 1)], pos_sem.at[0])
    for src, blk in ((0, ctx), (1, pair)):
        col = jnp.transpose(posb[blk])[:, :1]
        for r in range(2):
            qpos[src, r * rows : (r + 1) * rows, :] = col
    finish(1, dno_, upo_, far_)
    a3(2)
    start_y(3)
    y3(1)
    finish(1, faro_)
    keys_values(1)
    a1(3)
    kv_pair(0)
    y0(2)
    a2(3)
    finish(2, pair_, dn_, up_)
    y2(2)
    kv_relay(down_own, up_own, 0, 1)
    finish(2, dno_, upo_, far_)
    y3(2)
    finish(2, faro_)
    query(0)
    a3(3)
    units(0, 0, 0, 1)
    y0(3)
    kv_to_pair(1)
    add(3, own, first=True)
    finish(3, pair_, dn_, up_)
    kv_relay(down_oth, up_oth, 0, 6)
    kv_to_z(ctx, 1, 1)
    y2(3)
    units(0, 0, 1, 3)
    query_wait(0, 0)
    query_wait(0, 1)
    units(1, 0, 0, 1)
    y3(3)
    finish(3, dno_, upo_, far_)
    kv_pair(1)
    units(1, 0, 1, 2)
    finish(3, faro_)
    query(1)
    units(1, 0, 2, 3)
    far_wait(0)
    units(1, 0, 3, 4)
    give_back(0, 0)
    give_back(0, 1)
    kv_relay(down_own, up_own, 1, 1)
    units(0, 0, 3, 4)
    keep(0, 0)
    keep(0, 1)
    units(0, 1, 0, 1)
    kv_relay(down_oth, up_oth, 1, 6)
    units(0, 1, 1, 3)
    for r in range(2):
        query_wait(1, r)
        unit(1, 1, 0, halves[r])
    units(1, 1, 1, 3)
    far_wait(1)
    for r in range(2):
        unit(1, 1, 3, halves[r])
        give_back(1, r)
    for r in range(2):
        unit(0, 1, 3, halves[r])
        keep(1, r)
    mine = o_hbm.at[:, tile(par, 4 * hd)]
    pltpu.make_async_copy(mine, mine, out_sem.at[0]).wait()
    await_copy(o_hbm.at[:, tile(other, 4 * hd)], o_sem.at[0])
    for copy in sends[-SENDS:]:
        copy.wait_send()


def on_device(tokens, token_pos, norm_gain, query_weight, key_weight, value_weight):
    rows, feats = tokens.shape
    depth, nq = query_weight.shape
    nk = key_weight.shape[1]
    half = HEAD_DIM // 2
    freq = (10000.0 ** (-np.arange(half) * 2.0 / HEAD_DIM)).astype(np.float32)
    freq = jnp.asarray(np.concatenate([freq, freq])[None, :])
    hbm = pl.BlockSpec(memory_space=pl.ANY)
    bf16, f32 = jnp.bfloat16, jnp.float32
    dma = pltpu.SemaphoreType.DMA
    return pl.pallas_call(
        kernel,
        out_shape=jax.ShapeDtypeStruct((rows, nq), bf16),
        in_specs=[hbm] * 7,
        out_specs=hbm,
        scratch_shapes=[
            pltpu.VMEM((feats,), f32),
            pltpu.VMEM((1, HEAD_DIM), f32),
            pltpu.VMEM((rows,), jnp.int32),
            pltpu.VMEM((rows, HEAD_DIM), f32),
            pltpu.VMEM((rows, HEAD_DIM), f32),
            pltpu.VMEM((rows, feats), bf16),
            pltpu.VMEM((SHARDS, rows, depth), bf16),
            pltpu.VMEM((4, SHARDS, depth, nk), bf16),
            pltpu.VMEM((4, rows, nk), f32),
            pltpu.VMEM((SHARDS, 8, rows), f32),
            pltpu.VMEM((2, 2 * rows, 1), f32),
            pltpu.VMEM((SHARDS, 2, rows, 2 * HEAD_DIM), bf16),
            pltpu.VMEM((2, rows, 2 * HEAD_DIM), bf16),
            pltpu.VMEM((2, 2, 2 * rows, HEAD_DIM), bf16),
            pltpu.VMEM((2, 2 * rows, HEAD_DIM), bf16),
            pltpu.VMEM((2, 2, 2 * rows, 2 * HEAD_DIM), f32),
            pltpu.VMEM((4, rows, HEAD_DIM), bf16),
            pltpu.VMEM((4, rows, HEAD_DIM), bf16),
            dma((8,)),
            dma((1,)),
            dma((SENDS,)),
            dma((4, 16)),
            dma((2, 11)),
            dma((2, 2)),
            dma((1,)),
            dma((1,)),
        ],
        compiler_params=pltpu.CompilerParams(
            collective_id=0, has_side_effects=True, vmem_limit_bytes=62 * 1024 * 1024
        ),
        name="block",
    )(
        tokens, norm_gain, query_weight, key_weight, value_weight, freq, token_pos,
    )


def solution(mesh):
    in_specs = (
        P(("grp", "ctx"), None),
        P(("grp", "ctx")),
        P(),
        P("ctx", "tp"),
        P("ctx", "tp"),
        P("ctx", "tp"),
    )
    out_specs = P(("grp", "ctx"), "tp")
    return jax.shard_map(
        on_device, mesh=mesh, in_specs=in_specs, out_specs=out_specs, check_vma=False
    )
```

time: 104 us -> 99.4 us (0.956)
  Pallas kernels: 102 us -> 97 us
    pallas_call x1, Pallas kernels: 102 us -> 97 us  [on_device(): pl.pallas_call(kernel, out_shape=jax.ShapeDtypeStruct((rows, nq), bf16),...]
where the time goes in v4:
time: 99.4 us; the launch traced here: 99.3 us
  Pallas kernels  97 us (98%)
  local copies, waits for them, and re-layouts  2.26 us (2%)
    pallas_call x1, Pallas kernels, on_device(): pl.pallas_call(kernel, out_shape=jax.ShapeDtypeStruct((rows, nq), bf16),...  97 us
    unnamed x1, local copies, waits for them, and re-layouts  2.26 us

profile of v4, /device:TPU:1, one launch (start us, length us, event | category | flops | bytes accessed | tf_op | source)
XLA Modules:
  0.0 99.3 jit_solution(3786963257739982253)
XLA Ops:
  0.0 97.0 %block.1 = bf16[512,1024]{1,0:T(8,128)(2,1)} custom-call(bf16[512,4608]{1,0:T(8,128)(2,1)} %x_hbm.1, f32[4608]{0:T(1024)} %gain_hbm.1, bf16[576,1024]{1,0:T(8,128)(2,1)} %wq_hbm.1, bf16[576,512]{1,0:T(8,128)(2,1)} %wk_hbm.1, bf16[576,512]{1,0:T(8,128)(2,1)} %wv_hbm.1, f32[1,128]{1,0:T(1,128)} %constant.2.clone.freq_hbm, s32[512]{0:T(512)} %pos_hbm.1), custom_call_target="tpu_custom_call" | custom-call | tf_op jit(solution)/shard_map/block/pallas_call | solution.py:450
  97.0 2.3 %copy.9 = bf16[512,1024]{1,0:T(8,128)(2,1)} copy(bf16[512,1024]{1,0:T(8,128)(2,1)} %block.1) | data formatting | bytes 2097152

commit v5 on v4

--- a/solution.py
+++ b/solution.py
@@ -14,8 +14,8 @@
 query_scale = 144.0 ** (-0.5)
 EXP_SCALE = 50.0 * math.log2(math.e)
 SHARDS = 8
-SENDS = 32
-SPLITS = (144, 128, 112, 128)
+SENDS = 64
+SPLITS = (128, 112, 112, 112, 112)
 
 
 def tile(index, size):
@@ -66,19 +66,23 @@
                     j,
                 )
 
+    def load_q(j):
+        for r in range(2):
+            for i in range(2):
+                load(
+                    wq_hbm.at[:, pl.ds((4 * i + 2 * j + r) * hd, hd)],
+                    weights.at[2 + j, ctx, :, pl.ds((2 * r + i) * hd, hd)],
+                    2 + j,
+                )
+
     load_kv(0)
     load(x_hbm, xv, 4)
     load(gain_hbm, gain_ref, 5)
     load(pos_hbm, pos_ref, 6)
     load(freq_hbm, freq_ref, 7)
+    load_q(0)
     load_kv(1)
-    for j in range(2):
-        for i in range(2):
-            load(
-                wq_hbm.at[:, pl.ds((2 * i + j) * 2 * hd, 2 * hd)],
-                weights.at[2 + j, ctx, :, pl.ds(i * 2 * hd, 2 * hd)],
-                2 + j,
-            )
+    load_q(1)
     loaded(weights.at[0, ctx], 0)
     pl.semaphore_wait(barrier, SHARDS + 1)
 
@@ -90,12 +94,17 @@
             device_id=dev, device_id_type=MESH,
         )
 
+    def sent(at):
+        count, width = sends[at]
+        ref = weights.at[0, 0, pl.ds(0, count), pl.ds(0, width)]
+        copy_of(ref, ref, weight_sem.at[0, 0], to_peer, at).wait_send()
+
     def send(src, dst, recv, dev):
         if len(sends) >= SENDS:
-            sends[-SENDS].wait_send()
-        copy = copy_of(src, dst, recv, dev, len(sends))
-        copy.start()
-        sends.append(copy)
+            sent(len(sends) - SENDS)
+        copy_of(src, dst, recv, dev, len(sends)).start()
+        count, width = src.shape[-2:]
+        sends.append((count * src.dtype.itemsize // 2, width))
 
     def await_copy(dst, recv):
         copy_of(dst, dst, recv, to_peer, 0).wait_recv()
@@ -106,17 +115,20 @@
     down_own, down_oth = down * 2 + par, down * 2 + other
     far_own, far_oth = far * 2 + par, far * 2 + other
 
+    places = [(0, 0, nk), (2, 0, nk), (1, 0, nk), (3, 0, nk // 2), (3, nk // 2, nk // 2)]
+
     def add(p, *shards, first=False):
+        buf, start, count = places[p]
         width = 256
 
-        @pl.loop(0, nk // width)
+        @pl.loop(0, count // width)
         def _(i):
-            cols = tile(i, width)
+            cols = pl.ds(pl.multiple_of(start + i * width, width), width)
             part = sum(
-                jnp.dot(normed[s], weights[p, s, :, cols], preferred_element_type=jnp.float32)
+                jnp.dot(normed[s], weights[buf, s, :, cols], preferred_element_type=jnp.float32)
                 for s in shards
             )
-            acc[p, :, cols] = part if first else acc[p, :, cols] + part
+            acc[buf, :, cols] = part if first else acc[buf, :, cols] + part
 
     DN, UP, FAR, PAIR, DNO, UPO, FARO, PEER = 0, 2, 4, 5, 6, 7, 8, 9
     peer_role = [(down_own, 0), (up_own, 1), (far_own, 2), (pair, 3)]
@@ -125,10 +137,13 @@
     def part(p, shard, kind):
         base = core * (depth // 2) + (SPLITS[p] if kind else 0)
         size = depth // 2 - SPLITS[p] if kind else SPLITS[p]
-        return weights.at[p, shard, pl.ds(pl.multiple_of(base, 16), size), :]
+        buf, start, count = places[p]
+        return weights.at[buf, shard, pl.ds(pl.multiple_of(base, 16), size), pl.ds(start, count)]
 
     def side(p, shard, owner):
-        return weights.at[p, shard, pl.ds(pl.multiple_of(owner * (depth // 2), 16), depth // 2), :]
+        at = pl.ds(pl.multiple_of(owner * (depth // 2), 16), depth // 2)
+        buf, start, count = places[p]
+        return weights.at[buf, shard, at, pl.ds(start, count)]
 
     def send_part(p, shard, kind, role, dev):
         ref = part(p, shard, kind)
@@ -145,20 +160,24 @@
     def wait_side(p, shard, role):
         await_copy(side(p, shard, core), weight_sem.at[p, role])
 
+    to_y = (to_pair, to_cross)
+
     def a1(p):
-        wait_part(p, down_own, A, DN + A)
-        send_part(p, down_own, A, FAR, to_up)
-        send_part(p, down_own, A, DNO, to_pair)
-        wait_part(p, up_own, B, UP + B)
-        send_part(p, up_own, B, FAR, to_down)
-        send_part(p, up_own, B, UPO, to_cross)
+        low, high = p % 2, 1 - p % 2
+        wait_part(p, down_own, low, DN + low)
+        send_part(p, down_own, low, FAR, to_up)
+        send_part(p, down_own, low, DNO, to_y[low])
+        wait_part(p, up_own, high, UP + high)
+        send_part(p, up_own, high, FAR, to_down)
+        send_part(p, up_own, high, UPO, to_y[high])
 
     def a2(p):
-        wait_part(p, down_own, B, DN + B)
-        send_part(p, down_own, B, DNO, to_cross)
+        low, high = p % 2, 1 - p % 2
+        wait_part(p, down_own, high, DN + high)
+        send_part(p, down_own, high, DNO, to_y[high])
         to_other_core(p, 0)
-        wait_part(p, up_own, A, UP + A)
-        send_part(p, up_own, A, UPO, to_pair)
+        wait_part(p, up_own, low, UP + low)
+        send_part(p, up_own, low, UPO, to_y[low])
         to_other_core(p, 1)
 
     def a3(p):
@@ -181,11 +200,19 @@
         wait_side(p, far_oth, FARO)
         to_other_core(p, 6)
 
+    def first_z(p):
+        low, high = p % 2, 1 - p % 2
+        send_part(p, own, low, DN + low, to_up)
+        send_part(p, own, high, UP + high, to_down)
+
+    def second_z(p):
+        low, high = p % 2, 1 - p % 2
+        send_part(p, own, high, DN + high, to_up)
+        send_part(p, own, low, UP + low, to_down)
+
     def start_z(p):
-        send_part(p, own, A, DN + A, to_up)
-        send_part(p, own, B, UP + B, to_down)
-        send_part(p, own, B, DN + B, to_up)
-        send_part(p, own, A, UP + A, to_down)
+        first_z(p)
+        second_z(p)
 
     def start_y(p):
         send_part(p, own, A, PAIR, to_pair)
@@ -199,11 +226,12 @@
 
     dn_, up_, far_, pair_, dno_, upo_, faro_ = range(7)
 
-    start_z(0)
+    first_z(0)
     start_y(0)
+    second_z(0)
     loaded(pos_ref, 6)
     posb[ctx] = jnp.broadcast_to(pos_ref[...].reshape(1, rows), (8, rows)).astype(jnp.float32)
-    loaded(weights.at[1, ctx], 1)
+    loaded(weights.at[2, ctx], 2)
     start_y(1)
 
     loaded(xv, 4)
@@ -221,7 +249,7 @@
         for s in range(SHARDS):
             normed[s, at, :] = out[:, s * depth : (s + 1) * depth]
 
-    loaded(weights.at[2, ctx], 2)
+    loaded(weights.at[1, ctx], 1)
     loaded(weights.at[3, ctx], 3)
 
     def angles():
@@ -251,13 +279,12 @@
             ref[j, :, :hd] = rope(acc[j, :, tile(base, hd)]).astype(jnp.bfloat16)
             ref[j, :, hd:] = acc[j, :, tile(2 + base, hd)].astype(jnp.bfloat16)
 
-    def query(j):
-        for r in range(2):
-            at = slice(r * rows, (r + 1) * rows)
-            for ref, base in ((qx, other), (qb.at[0], par)):
-                u = acc[2 + j, :, tile(base * 2 + r, hd)]
-                ref[j, at, :] = (rope(u) * query_scale).astype(jnp.bfloat16)
-            send(qx.at[j, at, :], qb.at[1, j, at, :], q_sem.at[j, r], to_pair)
+    def query(j, r):
+        at = slice(r * rows, (r + 1) * rows)
+        for ref, base in ((qx, other), (qb.at[0], par)):
+            u = acc[2 + j, :, tile(2 * r + base, hd)]
+            ref[j, at, :] = (rope(u) * query_scale).astype(jnp.bfloat16)
+        send(qx.at[j, at, :], qb.at[1, j, at, :], q_sem.at[j, r], to_pair)
 
     def query_wait(j, r):
         at = slice(r * rows, (r + 1) * rows)
@@ -290,7 +317,7 @@
         await_copy(kv_half(low, j, 1), kv_sem.at[j, base + 1])
         await_copy(kv_half(high, j, 0), kv_sem.at[j, base + 2])
 
-    def unit(src, j, step, at=slice(None)):
+    def unit(src, j, step):
         zr = (z + step + step // 2 - 2 * (step // 3)) % 4
         blocks = pl.ds(zr * 2, 2)
         kk = kvb[blocks, j, :, :hd].reshape(2 * rows, hd)
@@ -298,19 +325,11 @@
         vv = jnp.concatenate([vv, jnp.ones_like(vv)], 1)
         kp = jnp.concatenate([posb[zr * 2, :1, :], posb[zr * 2 + 1, :1, :]], 1)
         s = lax.dot_general(
-            qb[src, j, at, :], kk, (((1,), (1,)), ((), ())), preferred_element_type=jnp.float32
+            qb[src, j], kk, (((1,), (1,)), ((), ())), preferred_element_type=jnp.float32
         )
         w = jnp.exp2(jnp.tanh(s * 0.02) * EXP_SCALE)
-        w = jnp.where(kp <= qpos[src, at, :], w, 0.0).astype(jnp.bfloat16)
-        num[src, j, at, :] += jnp.dot(w, vv, preferred_element_type=jnp.float32)
-
-    def units(src, j, first, last):
-        if last - first == 1:
-            unit(src, j, first)
-        else:
-            pl.loop(first, last)(lambda i: unit(src, j, i))
-
-    halves = [slice(r * rows, (r + 1) * rows) for r in range(2)]
+        w = jnp.where(kp <= qpos[src], w, 0.0).astype(jnp.bfloat16)
+        num[src, j] += jnp.dot(w, vv, preferred_element_type=jnp.float32)
 
     def result(src, j, r):
         n = num[src, j, r * rows : (r + 1) * rows, :]
@@ -356,13 +375,13 @@
     finish(0, dno_, upo_, far_)
     finish(0, faro_)
     keys_values(0)
+    a3(1)
     kv_to_pair(0)
-    a3(1)
+    kv_to_z(ctx, 0, 1)
     start_y(2)
     finish(1, dn_, up_)
     a1(2)
     start_z(3)
-    kv_to_z(ctx, 0, 1)
     y2(1)
     add(2, own, first=True)
     a2(2)
@@ -372,69 +391,108 @@
         for r in range(2):
             qpos[src, r * rows : (r + 1) * rows, :] = col
     finish(1, dno_, upo_, far_)
-    a3(2)
-    start_y(3)
     y3(1)
     finish(1, faro_)
-    keys_values(1)
-    a1(3)
-    kv_pair(0)
-    y0(2)
-    a2(3)
-    finish(2, pair_, dn_, up_)
-    y2(2)
+    query(0, 0)
+    query(0, 1)
     kv_relay(down_own, up_own, 0, 1)
-    finish(2, dno_, upo_, far_)
-    y3(2)
-    finish(2, faro_)
-    query(0)
-    a3(3)
-    units(0, 0, 0, 1)
-    y0(3)
-    kv_to_pair(1)
-    add(3, own, first=True)
-    finish(3, pair_, dn_, up_)
-    kv_relay(down_oth, up_oth, 0, 6)
-    kv_to_z(ctx, 1, 1)
-    y2(3)
-    units(0, 0, 1, 3)
-    query_wait(0, 0)
-    query_wait(0, 1)
-    units(1, 0, 0, 1)
-    y3(3)
-    finish(3, dno_, upo_, far_)
-    kv_pair(1)
-    units(1, 0, 1, 2)
-    finish(3, faro_)
-    query(1)
-    units(1, 0, 2, 3)
-    far_wait(0)
-    units(1, 0, 3, 4)
-    give_back(0, 0)
-    give_back(0, 1)
-    kv_relay(down_own, up_own, 1, 1)
-    units(0, 0, 3, 4)
-    keep(0, 0)
-    keep(0, 1)
-    units(0, 1, 0, 1)
-    kv_relay(down_oth, up_oth, 1, 6)
-    units(0, 1, 1, 3)
-    for r in range(2):
-        query_wait(1, r)
-        unit(1, 1, 0, halves[r])
-    units(1, 1, 1, 3)
-    far_wait(1)
-    for r in range(2):
-        unit(1, 1, 3, halves[r])
-        give_back(1, r)
-    for r in range(2):
-        unit(0, 1, 3, halves[r])
-        keep(1, r)
+
+    def before_0():
+        kv_pair(0)
+
+    def before_1():
+        start_y(3)
+        y0(2)
+        a3(2)
+        finish(2, pair_, dn_, up_)
+        a1(3)
+        a2(3)
+        start_z(4)
+        start_y(4)
+        y2(2)
+        finish(2, dno_, upo_, far_)
+        query_wait(0, 0)
+        query_wait(0, 1)
+
+    def before_2():
+        kv_relay(down_oth, up_oth, 0, 6)
+        y0(3)
+
+    def before_3():
+        a3(3)
+        y3(2)
+        a1(4)
+        finish(2, faro_)
+        keys_values(1)
+        kv_to_pair(1)
+        a2(4)
+
+    def before_4():
+        kv_to_z(ctx, 1, 1)
+        add(3, own, first=True)
+        finish(3, pair_, dn_, up_)
+        y2(3)
+
+    def before_5():
+        a3(4)
+        y3(3)
+        finish(3, dno_, upo_, far_)
+        add(4, own, first=True)
+        y0(4)
+        finish(3, faro_)
+        query(1, 0)
+        finish(4, pair_, dn_, up_)
+        y2(4)
+        y3(4)
+        kv_pair(1)
+        finish(4, dno_, upo_, far_)
+        finish(4, faro_)
+        query(1, 1)
+
+    def before_6():
+        kv_relay(down_own, up_own, 1, 1)
+        far_wait(0)
+
+    def before_7():
+        give_back(0, 0)
+        give_back(0, 1)
+
+    def before_8():
+        keep(0, 0)
+        keep(0, 1)
+
+    def before_9():
+        kv_relay(down_oth, up_oth, 1, 6)
+        query_wait(1, 0)
+        query_wait(1, 1)
+
+    def before_13():
+        give_back(1, 0)
+        give_back(1, 1)
+
+    before = {
+        0: before_0, 1: before_1, 2: before_2, 3: before_3, 4: before_4, 5: before_5,
+        6: before_6, 7: before_7, 8: before_8, 9: before_9,
+        12: lambda: far_wait(1), 13: before_13,
+    }
+
+    @pl.loop(0, 16)
+    def _(t):
+        for at, action in before.items():
+            pl.when(t == at)(action)
+        j, u = t // 8, t % 8
+        past = (u + 3) // 8
+        late = (u + 3) // 4 - 2 * past
+        theirs = (1 - j) * ((u % 2 + u // 6) % 2) + j * late
+        unit(theirs, j, (1 - j) * (u // 2) + j * (u - late - 4 * past))
+
+    keep(1, 0)
+    keep(1, 1)
     mine = o_hbm.at[:, tile(par, 4 * hd)]
     pltpu.make_async_copy(mine, mine, out_sem.at[0]).wait()
     await_copy(o_hbm.at[:, tile(other, 4 * hd)], o_sem.at[0])
-    for copy in sends[-SENDS:]:
-        copy.wait_send()
+    for at in range(len(sends) - SENDS, len(sends)):
+        sent(at)
 
 
 def on_device(tokens, token_pos, norm_gain, query_weight, key_weight, value_weight):
@@ -474,7 +532,7 @@
             dma((8,)),
             dma((1,)),
             dma((SENDS,)),
-            dma((4, 16)),
+            dma((5, 16)),
             dma((2, 11)),
             dma((2, 2)),
             dma((1,)),

time: 99.4 us -> 97.7 us (0.983)
  Pallas kernels: 97 us -> 95.1 us
    pallas_call x1, Pallas kernels: 97 us -> 95.1 us  [on_device(): pl.pallas_call(kernel, out_shape=jax.ShapeDtypeStruct((rows, nq), bf16),...]
where the time goes in v5:
time: 97.7 us; the launch traced here: 97.4 us
  Pallas kernels  95.1 us (97%)
  local copies, waits for them, and re-layouts  2.26 us (2%)
    pallas_call x1, Pallas kernels, on_device(): pl.pallas_call(kernel, out_shape=jax.ShapeDtypeStruct((rows, nq), bf16),...  95.1 us
    unnamed x1, local copies, waits for them, and re-layouts  2.26 us

profile of v5, /device:TPU:1, one launch (start us, length us, event | category | flops | bytes accessed | tf_op | source)
XLA Modules:
  0.0 97.4 jit_solution(10572384588665418046)
XLA Ops:
  0.0 95.1 %block.1 = bf16[512,1024]{1,0:T(8,128)(2,1)} custom-call(bf16[512,4608]{1,0:T(8,128)(2,1)} %x_hbm.1, f32[4608]{0:T(1024)} %gain_hbm.1, bf16[576,1024]{1,0:T(8,128)(2,1)} %wq_hbm.1, bf16[576,512]{1,0:T(8,128)(2,1)} %wk_hbm.1, bf16[576,512]{1,0:T(8,128)(2,1)} %wv_hbm.1, f32[1,128]{1,0:T(1,128)} %constant.2.clone.freq_hbm, s32[512]{0:T(512)} %pos_hbm.1), custom_call_target="tpu_custom_call" | custom-call | tf_op jit(solution)/shard_map/block/pallas_call | solution.py:508
  95.1 2.3 %copy.9 = bf16[512,1024]{1,0:T(8,128)(2,1)} copy(bf16[512,1024]{1,0:T(8,128)(2,1)} %block.1) | data formatting | bytes 2097152

commit v6 on v5

--- a/solution.py
+++ b/solution.py
@@ -425,10 +425,10 @@
         finish(2, faro_)
         keys_values(1)
         kv_to_pair(1)
+        kv_to_z(ctx, 1, 1)
         a2(4)
 
     def before_4():
-        kv_to_z(ctx, 1, 1)
         add(3, own, first=True)
         finish(3, pair_, dn_, up_)
         y2(3)

time: 97.7 us -> 97.7 us (level)
  no operation moved by 1% of the time
where the time goes in v6:
time: 97.7 us; the launch traced here: 97.4 us
  Pallas kernels  95.1 us (97%)
  local copies, waits for them, and re-layouts  2.26 us (2%)
    pallas_call x1, Pallas kernels, on_device(): pl.pallas_call(kernel, out_shape=jax.ShapeDtypeStruct((rows, nq), bf16),...  95.1 us
    unnamed x1, local copies, waits for them, and re-layouts  2.26 us

profile of v6, /device:TPU:1, one launch (start us, length us, event | category | flops | bytes accessed | tf_op | source)
XLA Modules:
  0.0 97.4 jit_solution(2904104881203949259)
XLA Ops:
  0.0 95.1 %block.1 = bf16[512,1024]{1,0:T(8,128)(2,1)} custom-call(bf16[512,4608]{1,0:T(8,128)(2,1)} %x_hbm.1, f32[4608]{0:T(1024)} %gain_hbm.1, bf16[576,1024]{1,0:T(8,128)(2,1)} %wq_hbm.1, bf16[576,512]{1,0:T(8,128)(2,1)} %wk_hbm.1, bf16[576,512]{1,0:T(8,128)(2,1)} %wv_hbm.1, f32[1,128]{1,0:T(1,128)} %constant.2.clone.freq_hbm, s32[512]{0:T(512)} %pos_hbm.1), custom_call_target="tpu_custom_call" | custom-call | tf_op jit(solution)/shard_map/block/pallas_call | solution.py:508
  95.1 2.3 %copy.9 = bf16[512,1024]{1,0:T(8,128)(2,1)} copy(bf16[512,1024]{1,0:T(8,128)(2,1)} %block.1) | data formatting | bytes 2097152

commit v7 on v6

--- a/solution.py
+++ b/solution.py
@@ -15,7 +15,7 @@
 EXP_SCALE = 50.0 * math.log2(math.e)
 SHARDS = 8
 SENDS = 64
-SPLITS = (128, 112, 112, 112, 112)
+SPLITS = (128, 112, 96, 112, 112)
 
 
 def tile(index, size):

time: 97.7 us -> 98 us (level)
  no operation moved by 1% of the time
where the time goes in v7:
time: 98 us; the launch traced here: 97.8 us
  Pallas kernels  95.6 us (98%)
  local copies, waits for them, and re-layouts  2.26 us (2%)
    pallas_call x1, Pallas kernels, on_device(): pl.pallas_call(kernel, out_shape=jax.ShapeDtypeStruct((rows, nq), bf16),...  95.6 us
    unnamed x1, local copies, waits for them, and re-layouts  2.26 us

profile of v7, /device:TPU:1, one launch (start us, length us, event | category | flops | bytes accessed | tf_op | source)
XLA Modules:
  0.0 97.8 jit_solution(11409993178333224365)
XLA Ops:
  0.0 95.6 %block.1 = bf16[512,1024]{1,0:T(8,128)(2,1)} custom-call(bf16[512,4608]{1,0:T(8,128)(2,1)} %x_hbm.1, f32[4608]{0:T(1024)} %gain_hbm.1, bf16[576,1024]{1,0:T(8,128)(2,1)} %wq_hbm.1, bf16[576,512]{1,0:T(8,128)(2,1)} %wk_hbm.1, bf16[576,512]{1,0:T(8,128)(2,1)} %wv_hbm.1, f32[1,128]{1,0:T(1,128)} %constant.2.clone.freq_hbm, s32[512]{0:T(512)} %pos_hbm.1), custom_call_target="tpu_custom_call" | custom-call | tf_op jit(solution)/shard_map/block/pallas_call | solution.py:508
  95.6 2.3 %copy.9 = bf16[512,1024]{1,0:T(8,128)(2,1)} copy(bf16[512,1024]{1,0:T(8,128)(2,1)} %block.1) | data formatting | bytes 2097152
